TPU v7x, 512 devices: a 8x2x16 block of a 8x8x16 slice. The times are simulated.
512 devices in a mesh: rep: 2 (over y), seq: 128 (over x, z), head: 2 (over core).
Axes of the slice: x: 8, y: 2, z: 16, core: 2. Of those that a mesh axis runs over, the one named last changes fastest.
The devices are a block of a 8x8x16 slice.
Arguments:
- prompt_query: bfloat16 [32768, 1792], P(('rep', 'seq', 'head')), parts along dimension 0, may hold values from -12 to 12
- prompt_key: bfloat16 [32768, 256], P(('rep', 'seq', 'head')), parts along dimension 0, may hold values from -12 to 12
- prompt_value: bfloat16 [32768, 256], P(('rep', 'seq', 'head')), parts along dimension 0, may hold values from -24 to 24
- prompt_length: int32 [2], P('rep'), parts along dimension 0, may hold values from 8192 to 16384
- span_order: int32 [512], P('rep'), parts along dimension 0, may hold values from 0 to 255, each once
- new_query: bfloat16 [32, 1792], P('rep', 'head'), parts along dimension 0, may hold values from -12 to 12
- new_key: bfloat16 [32, 256], P('rep', 'head'), parts along dimension 0, may hold values from -12 to 12
- new_value: bfloat16 [32, 256], P('rep', 'head'), parts along dimension 0, may hold values from -24 to 24
- cache_key: bfloat16 [32, 2, 32768, 128], P('rep', 'head', 'seq'), parts along dimension 0, may hold values from -12 to 12
- cache_value: bfloat16 [32, 2, 32768, 128], P('rep', 'head', 'seq'), parts along dimension 0, may hold values from -24 to 24
- cache_length: int32 [32], P('rep'), parts along dimension 0, may hold values from 16640 to 32768
Outputs:
- prompt_attended: bfloat16 [32768, 1792], P(('rep', 'seq', 'head')), parts along dimension 0
- decode_attended: bfloat16 [32, 1792], P('rep', 'head'), parts along dimension 0
There are 2 independent parts, one for each index of `rep`. A program takes and returns all parts, laid end to end along the dimension named above; each array names one. Nothing has to cross between parts.
Inputs may be any that keep to these rules, and one draw needn't show every extreme that they name: `span_order`: each of the 256 spans stands once.
All inputs are finite; a program needn't handle non-finite values.
Results may differ from a plain program's by a relative error of at most 0.0045.
Values may be sent and summed in bfloat16 or wider, within the bound.
A program may use at most 128 MiB of HBM per device.

v0:
```python
import math

import jax
import jax.numpy as jnp
from jax import lax
from jax.sharding import Mesh
from jax.sharding import PartitionSpec as P

HD = 128
QH = 14
KVH = 2
SEQ = ("seq_0", "seq_1")
SEQ_HEAD = ("seq_0", "seq_1", "head")
REP_SEQ_HEAD = ("rep", "seq_0", "seq_1", "head")


def side_by_side(arrays, axis, dim, along):
    both = jnp.concatenate(arrays, axis=along)
    out, at, gathered = (lax.all_gather(both, axis, axis=dim, tiled=True), 0, [])
    for a in arrays:
        gathered.append(lax.slice_in_dim(out, at, at + a.shape[along], axis=along))
        at += a.shape[along]
    return tuple(gathered)


def gathered_once(array, axis):
    leaves = jax.tree.leaves(array)
    order = sorted(range(len(leaves)), key=lambda k: -leaves[k].size)
    width = (1, *leaves[order[0]].shape)[-1]
    lines = [
        jnp.pad(leaves[k].reshape(-1), (0, -leaves[k].size % width)).reshape(-1, width)
        for k in order
    ]
    both, at, found = (lax.all_gather(jnp.concatenate(lines), axis), 0, {})
    for k, line in zip(order, lines):
        piece = both[:, at : at + len(line)].reshape(len(both), -1)
        found[k] = piece[:, : leaves[k].size].reshape(-1, *leaves[k].shape)
        at += len(line)
    numbers = iter(range(len(leaves)))
    return jax.tree.map(lambda _: found[next(numbers)], array)


def combined_by_axis(array, axes, combine):
    for axis in axes:
        pieces = gathered_once(array, axis)
        array = jax.tree.map(lambda part: part[0], pieces)
        for k in range(1, lax.axis_size(axis)):
            array = combine(array, jax.tree.map(lambda part: part[k], pieces))
    return array


def lookup(span_table, row_ids, span_rows):
    chosen = (
        row_ids[:, None] // span_rows == jnp.arange(span_table.shape[0], dtype=jnp.int32)[None, :]
    )
    picked = jnp.sum(jnp.where(chosen, span_table[None, :], 0), axis=1)
    return picked * span_rows + row_ids % span_rows


def block_size(key_count, span_rows):
    units = key_count // span_rows
    most = max(1, 512 // span_rows)
    best = 1
    for count in range(1, min(units, most) + 1):
        if units % count == 0:
            best = count
    return best * span_rows


def start_state(query_rows, kv_heads, head_group):
    row_max = jnp.full((kv_heads, head_group, query_rows), -1e30, jnp.float32)
    row_total = jnp.zeros((kv_heads, head_group, query_rows), jnp.float32)
    weighted = jnp.zeros((kv_heads, head_group, query_rows, HD), jnp.float32)
    return (row_max, row_total, weighted)


def attend_rows(running, shard_piece, queries, query_pos, span_table, span_rows, length_limit):
    keys_piece, values_piece = shard_piece
    key_count = keys_piece.shape[0]
    kv_heads = queries.shape[1]
    block_rows = block_size(key_count, span_rows)
    score_scale = 1.0 / math.sqrt(HD)

    def advance(carried, block_index):
        first_row = block_index * block_rows
        key_block = lax.dynamic_slice_in_dim(keys_piece, first_row, block_rows, 0).reshape(
            block_rows, kv_heads, HD
        )
        value_block = lax.dynamic_slice_in_dim(values_piece, first_row, block_rows, 0).reshape(
            block_rows, kv_heads, HD
        )
        key_pos = lookup(span_table, first_row + jnp.arange(block_rows, dtype=jnp.int32), span_rows)
        allowed = (key_pos[None, :] <= query_pos[:, None]) & (key_pos[None, :] < length_limit)

        def compute(state_in):
            row_max, row_total, weighted = state_in
            scores = (
                jnp.einsum("rkgd,nkd->kgrn", queries, key_block, preferred_element_type=jnp.float32)
                * score_scale
            )
            scores = jnp.where(allowed, scores, -1e30)
            new_max = jnp.maximum(row_max, jnp.max(scores, axis=-1))
            weights = jnp.where(allowed, jnp.exp(scores - new_max[..., None]), 0.0)
            factor = jnp.exp(row_max - new_max)
            row_total = row_total * factor + jnp.sum(weights, axis=-1)
            weighted = weighted * factor[..., None] + jnp.einsum(
                "kgrn,nkd->kgrd",
                weights.astype(jnp.bfloat16),
                value_block,
                preferred_element_type=jnp.float32,
            )
            return (new_max, row_total, weighted)

        return (lax.cond(jnp.any(allowed), compute, lambda state_in: state_in, carried), None)

    running, _ = lax.scan(advance, running, jnp.arange(key_count // block_rows, dtype=jnp.int32))
    return running


def finish(running, query_pos, length_limit):
    row_max, row_total, weighted = running
    result = weighted / row_total[..., None]
    result = jnp.transpose(result, (2, 0, 1, 3))
    result = jnp.where((query_pos < length_limit)[:, None, None, None], result, 0.0)
    return result.reshape(result.shape[0], -1).astype(jnp.bfloat16)


def combine_parts(left, right):
    left_max, left_total, left_weighted = left
    right_max, right_total, right_weighted = right
    joint = jnp.maximum(left_max, right_max)
    left_factor = jnp.exp(left_max - joint)
    right_factor = jnp.exp(right_max - joint)
    return (
        joint,
        left_total * left_factor + right_total * right_factor,
        left_weighted * left_factor[..., None] + right_weighted * right_factor[..., None],
    )


def per_device(
    prompt_query,
    prompt_key,
    prompt_value,
    prompt_length,
    span_order,
    new_query,
    new_key,
    new_value,
    cache_key,
    cache_value,
    cache_length,
):
    head_group = QH // KVH
    score_scale = 1.0 / math.sqrt(HD)
    length_limit = prompt_length[0]
    span_rows = prompt_query.shape[0]
    kv_heads = prompt_key.shape[1] // HD
    first_row = (lax.axis_index(SEQ) * lax.axis_size("head") + lax.axis_index("head")) * span_rows
    query_pos = lookup(span_order, first_row + jnp.arange(span_rows, dtype=jnp.int32), span_rows)
    queries = prompt_query.reshape(span_rows, kv_heads, head_group, HD)
    running = attend_rows(
        start_state(span_rows, kv_heads, head_group),
        side_by_side((prompt_key, prompt_value), SEQ_HEAD, 0, 1),
        queries,
        query_pos,
        span_order,
        span_rows,
        length_limit,
    )
    prompt_attended = finish(running, query_pos, length_limit)
    sessions = new_query.shape[0]
    local_heads = cache_key.shape[1]
    local_ctx = cache_key.shape[2]
    dec_queries = new_query.reshape(sessions, local_heads, head_group, HD)
    cache_pos = lax.axis_index(SEQ) * local_ctx + jnp.arange(local_ctx, dtype=jnp.int32)
    valid = (cache_pos[None, :] < cache_length[:, None])[:, None, None, :]
    scores = (
        jnp.einsum("skgd,sktd->skgt", dec_queries, cache_key, preferred_element_type=jnp.float32)
        * score_scale
    )
    scores = jnp.where(valid, scores, -1e30)
    row_max = jnp.max(scores, axis=-1)
    weights = jnp.where(valid, jnp.exp(scores - row_max[..., None]), 0.0)
    row_total = jnp.sum(weights, axis=-1)
    weighted = jnp.einsum(
        "skgt,sktd->skgd",
        weights.astype(jnp.bfloat16),
        cache_value,
        preferred_element_type=jnp.float32,
    )
    row_max, row_total, weighted = combined_by_axis(
        (row_max, row_total, weighted), SEQ, combine_parts
    )
    own_score = (
        jnp.einsum(
            "skgd,skd->skg",
            dec_queries,
            new_key.reshape(sessions, local_heads, HD),
            preferred_element_type=jnp.float32,
        )
        * score_scale
    )
    final_max = jnp.maximum(row_max, own_score)
    old_factor = jnp.exp(row_max - final_max)
    own_weight = jnp.exp(own_score - final_max)
    row_total = row_total * old_factor + own_weight
    own_rounded = lax.optimization_barrier(own_weight.astype(jnp.bfloat16)).astype(jnp.float32)
    fresh_value = new_value.reshape(sessions, local_heads, 1, HD).astype(jnp.float32)
    weighted = weighted * old_factor[..., None] + own_rounded[..., None] * fresh_value
    decode_attended = (weighted / row_total[..., None]).reshape(sessions, -1).astype(jnp.bfloat16)
    return (prompt_attended, decode_attended)


def solution(mesh):
    finer = Mesh(
        mesh.devices.reshape(mesh.shape["rep"], 8, 16, mesh.shape["head"]),
        ("rep", "seq_0", "seq_1", "head"),
    )
    placed = (
        P(REP_SEQ_HEAD, None),
        P(REP_SEQ_HEAD, None),
        P(REP_SEQ_HEAD, None),
        P("rep"),
        P("rep"),
        P("rep", "head"),
        P("rep", "head"),
        P("rep", "head"),
        P("rep", "head", SEQ, None),
        P("rep", "head", SEQ, None),
        P("rep"),
    )
    return jax.shard_map(
        per_device,
        mesh=finer,
        in_specs=placed,
        out_specs=(P(REP_SEQ_HEAD, None), P("rep", "head")),
        check_vma=False,
    )
```

profile of v0, /device:TPU:65, one launch (start us, length us, event | category | flops | bytes accessed | tf_op | source)
XLA Modules:
  0.0 460.3 jit_solution(7138965110264007469)
XLA Ops:
  12.8 21.5 %all-gather.2 = f32[8,114,128]{2,1,0:T(8,128)S(1)} all-gather(f32[1,114,128]{2,1,0:T(8,128)S(1)} %maximum_bitcast_fusion), channel_id=2, replica_groups=mesh['rep'=2,'seq_0'=8,'seq_1'=16,'head'=2] {'seq_0'}, dimensions={0}, use_global_device_ids=true | all-gather | bytes 525312 | tf_op jit(solution)/shard_map/all_gather | solution.py:34
  34.7 70.1 %all-gather.3 = f32[16,114,128]{2,1,0:T(8,128)S(1)} all-gather(f32[1,114,128]{2,1,0:T(8,128)S(1)} %maximum_bitcast_fusion.1), channel_id=3, replica_groups=mesh['rep'=2,'seq_0'=8,'seq_1'=16,'head'=2] {'seq_1'}, dimensions={0}, use_global_device_ids=true | all-gather | bytes 992256 | tf_op jit(solution)/shard_map/all_gather | solution.py:34
  113.9 87.8 %all-gather.6.cloned.1.call-done = bf16[16384,512]{1,0:T(8,128)(2,1)} async-done(((bf16[64,512]{1,0:T(8,128)(2,1)}), bf16[16384,512]{1,0:T(8,128)(2,1)}) %all-gather.6.cloned.1.call-update) | async-done | bytes 16777232 | tf_op jit(solution)/shard_map/all_gather | solution.py:19
  201.6 11.3 %fusion.103 = (bf16[16384,256]{1,0:T(8,128)(2,1)}, bf16[16384,256]{1,0:T(8,128)(2,1)}) fusion(bf16[16384,512]{1,0:T(8,128)(2,1)} %all-gather.6.cloned.1.call-done), kind=kLoop, calls=%fused_computation.273 | loop fusion | bytes 33554432 | tf_op jit(solution)/shard_map/slice | solution.py:21
  212.9 11.9 %copy.34 = bf16[16384,256]{0,1:T(8,128)(2,1)} copy(bf16[16384,256]{1,0:T(8,128)(2,1)} %get-tuple-element.415) | data formatting | bytes 16777216 | tf_op jit(solution)/shard_map/while | solution.py:116
  224.8 12.0 %copy.36 = bf16[16384,256]{0,1:T(8,128)(2,1)} copy(bf16[16384,256]{1,0:T(8,128)(2,1)} %get-tuple-element.414) | data formatting | bytes 16777216 | tf_op jit(solution)/shard_map/while | solution.py:116
  236.8 215.3 %while.16 = (s32[]{:T(128)}, f32[2,7,64]{2,1,0:T(8,128)S(1)}, f32[2,7,64]{2,1,0:T(8,128)S(1)}, f32[2,7,64,128]{3,2,1,0:T(8,128)S(1)}, s32[32]{0:T(128)S(1)}, /*i...) while((s32[]{:T(128)}, f32[2,7,64]{2,1,0:T(8,128)S(1)}, ...), condition=%wide.region_8.9_spmd, body=%wide.region_1.8_spmd.sunk | while | flops 241582848 | bytes 8428101 | solution.py:116
  240.3 3.3 conditional.2
  247.0 3.3 conditional.2
  253.7 3.3 conditional.2
  260.5 3.3 conditional.2
  267.2 3.3 conditional.2
  273.9 3.3 conditional.2
  280.7 3.3 conditional.2
  287.4 3.3 conditional.2
  294.1 3.3 conditional.2
  300.9 3.3 conditional.2
  307.6 3.3 conditional.2
  314.3 3.3 conditional.2
  321.0 3.3 conditional.2
  327.8 3.3 conditional.2
  334.5 3.3 conditional.2
  341.2 3.3 conditional.2
  347.9 3.3 conditional.2
  354.7 3.3 conditional.2
  361.4 3.3 conditional.2
  368.1 3.3 conditional.2
  374.9 3.3 conditional.2
  381.6 3.3 conditional.2
  388.3 3.3 conditional.2
  395.0 3.3 conditional.2
  408.5 3.3 conditional.2
  (527 shorter events, 211.4 us)
Async XLA Ops:
  7.2 3.2 copy-start
  7.2 194.4 %all-gather.6.cloned.1.call-start = ((), (), s32[]{:S(2)}) async-start(), calls=%async_computation | async-start | bytes 16842752 | tf_op jit(solution)/shard_map/all_gather | solution.py:19
  104.8 3.4 copy-start.4
  104.8 3.8 copy-start.3
  104.9 4.4 copy-start.1
  104.9 4.8 %copy-start.2 = (s32[256]{0:T(256)S(1)}, s32[256]{0:T(256)}, u32[]{:S(2)}) copy-start(s32[256]{0:T(256)} %param.19) | copy-start | bytes 3076
Sparse Core Ops, SparseCore 0:
  11.8 189.8 all-gather.5
where the time goes:
time: 463 us; the launch traced here: 460 us
  local copies, waits for them, and re-layouts  106 us (23%)
  blocking collectives  91.7 us (20%)
  waiting for transfers between devices  87.8 us (19%)
  other arithmetic  76.8 us (17%)
  loops' own time  41.9 us (9%)
  matrix products  41.2 us (9%)
  between operations  15.1 us (3%)
    all_gather x2, blocking collectives, gathered_once(): both, at, found = (lax.all_gather(jnp.concatenate(lines), axis), 0, {})  91.7 us
    all_gather x1, waiting for transfers between devices, side_by_side(): lax.all_gather(both, axis, axis=dim, tiled=True)  87.8 us
    dynamic_slice x32, local copies, waits for them, and re-layouts, advance(): lax.dynamic_slice_in_dim(values_piece, first_row, block_rows, 0)  43 us
    another operation x1, loops' own time, attend_rows(): lax.scan(advance, running, jnp.arange(key_count // block_rows, dtype=jnp....  40.1 us
    while x3, local copies, waits for them, and re-layouts, attend_rows(): lax.scan(advance, running, jnp.arange(key_count // block_rows, dtype=jnp....  23.9 us
    dot_general x32, matrix products, compute(): jnp.einsum('kgrn,nkd->kgrd', weights.astype(jnp.bfloat16), value_block, p...  23.8 us
    and x32, other arithmetic, advance(): (key_pos[None, :] <= query_pos[:, None]) & (key_pos[None, :] < length_limit)  23.2 us
    lt x32, other arithmetic, advance(): key_pos[None, :] < length_limit  21.2 us
  transfers between devices with their start and end apart: 1, of which 1 were waited for; matrix products, arithmetic and copies ran while one was open for 3% of the time, Pallas kernels for 0%

commit v1 on v0

v1 whole, which is shorter than its diff:
```python
import heapq
import math

import jax
import jax.numpy as jnp
import numpy as np
from jax import lax
from jax.experimental import pallas as pl
from jax.experimental.pallas import tpu as pltpu
from jax.sharding import Mesh
from jax.sharding import PartitionSpec as P

HD = 128
QH = 14
KVH = 2
GROUP = QH // KVH
SEQ = ("seq_0", "seq_1")
REP_SEQ_HEAD = ("rep", "seq_0", "seq_1", "head")
TILE = 8
NEG = -1e30
MESH = pl.DeviceIdType.MESH


def build_flow(n1, n2):
    half1, half2 = n1 // 2, n2 // 2
    members = {0: [0], half1: [-half1]}
    for k in range(1, half1):
        members[k] = [-k, k]
    heap, free, seq, arrived = [], {}, [0], {}
    order, first, sends = [], [], {}

    def send(now, link, item, into):
        units = len(members[item[2]]) if item[0] == 2 else 1
        begin = max(now, free.get(link, 0.0))
        free[link] = begin + units * (0.75 if link[0] == 2 else 1.4)
        seq[0] += 1
        heapq.heappush(heap, (free[link] + 2.5, seq[0], item))
        into.append(item)

    def phase2(now, k, into):
        for way in (1, -1):
            send(now, (2, way), (2, way, k, -way), into)

    for way in (1, -1):
        send(0.0, (1, way), (1, way, -way, 0), first)
    phase2(0.0, 0, first)
    groups = [(0, 0)]
    while heap:
        now, _, item = heapq.heappop(heap)
        order.append(item)
        into = sends.setdefault(item, [])
        ring, way, which, off2 = item
        if ring == 1:
            dist, k = abs(which), abs(which)
            if dist + 1 <= (half1 if way == 1 else half1 - 1):
                send(now, (1, way), (1, way, which - way, 0), into)
            arrived[k] = arrived.get(k, 0) + 1
            if arrived[k] == len(members[k]):
                groups.append((k, 0))
                phase2(now, k, into)
        else:
            dist = abs(off2)
            groups.append((which, off2))
            last = dist + 1 == half2 and way == (1 if which % 2 == 0 else -1)
            if dist + 1 < half2 or last:
                send(now, (2, way), (2, way, which, off2 - way), into)
    slot, offsets = {}, []
    for k, off2 in groups:
        slot[(k, off2)] = len(offsets)
        offsets.extend((m, off2) for m in members[k])

    def place(item):
        ring, _, which, off2 = item
        if ring == 2:
            return slot[(which, off2)], len(members[which])
        return slot[(abs(which), 0)] + members[abs(which)].index(which), 1

    number = {item: i for i, item in enumerate(order)}

    def resolve(items):
        out = []
        for item in items:
            ring, way, which, off2 = item
            source = (1, way, which + way, 0) if ring == 1 else (2, way, which, off2 + way)
            if ring == 1 and source[2] == 0:
                src = slot[(0, 0)]
            else:
                src = place(source)[0]
            dst, count = place(item)
            out.append((ring, way, src, dst, count, number[item]))
        return out

    steps, total = [], len(offsets) // TILE
    events = [(place(item), resolve(sends[item]), number[item]) for item in order]
    at, filled = 0, {0}
    for tile in range(total):
        need = set(range(tile * TILE, (tile + 1) * TILE))
        mine = []
        while not need <= filled:
            (dst, count), todo, sem = events[at]
            filled.update(range(dst, dst + count))
            mine.append((dst, count, todo, sem))
            at += 1
        steps.append(mine)
    assert at == len(events) and len(offsets) == n1 * n2
    return offsets, resolve(first), steps, len(events)


def prompt_kernel(
    flows,
    sizes,
    span_ref,
    limit_ref,
    q_ref,
    bias_ref,
    k_ref,
    v_ref,
    out_ref,
    buf,
    q_s,
    acc,
    top,
    tot,
    local_sem,
    recv_sem,
    send_sem,
    pair_recv,
    pair_send,
):
    n_x, n_z = sizes
    rows = q_ref.shape[0]
    x, z, core = lax.axis_index("seq_0"), lax.axis_index("seq_1"), lax.axis_index("head")
    steps = len(flows[0][2])
    names = ("seq_0", "seq_1")
    here = (x, z)
    extent = (n_x, n_z)

    def target(dim, way):
        return {names[dim]: lax.rem(here[dim] + way + extent[dim], extent[dim])}

    partner = {"head": 1 - core}
    in_k = pltpu.make_async_copy(k_ref, buf.at[0, 0, :, : KVH * HD], local_sem.at[0])
    in_v = pltpu.make_async_copy(v_ref, buf.at[0, 0, :, KVH * HD :], local_sem.at[1])
    in_k.start()
    in_v.start()
    barrier = pltpu.get_barrier_semaphore()
    for dim in (0, 1):
        for way in (1, -1):
            pl.semaphore_signal(barrier, inc=1, device_id=target(dim, way), device_id_type=MESH)
    pl.semaphore_signal(barrier, inc=1, device_id=partner, device_id_type=MESH)
    in_k.wait()
    in_v.wait()
    pl.semaphore_wait(barrier, 5)

    def ring_copy(flow, send):
        ring, way, src, dst, count, sem = send
        dim = (ring - 1) if flow == 0 else (2 - ring)
        return pltpu.make_async_remote_copy(
            src_ref=buf.at[0, pl.ds(src, count)],
            dst_ref=buf.at[0, pl.ds(dst, count)],
            send_sem=send_sem.at[0],
            recv_sem=recv_sem.at[sem],
            device_id=target(dim, way),
            device_id_type=MESH,
        )

    def pair_copy(tile):
        return pltpu.make_async_remote_copy(
            src_ref=buf.at[0, pl.ds(tile * TILE, TILE)],
            dst_ref=buf.at[1, pl.ds(tile * TILE, TILE)],
            send_sem=pair_send.at[0],
            recv_sem=pair_recv.at[tile],
            device_id=partner,
            device_id_type=MESH,
        )

    for flow in (0, 1):

        @pl.when(core == flow)
        def _():
            for send in flows[flow][1]:
                ring_copy(flow, send).start()

    scale = math.log2(math.e) / math.sqrt(HD)

    row = lax.broadcasted_iota(jnp.int32, (rows, rows), 0)
    col = lax.broadcasted_iota(jnp.int32, (rows, rows), 1)
    tri = jnp.concatenate([jnp.where(col <= row, 0.0, NEG).astype(jnp.float32)] * GROUP, axis=0)
    for g in range(KVH):
        for h in range(GROUP):
            head = g * GROUP + h
            q_s[g, h * rows : (h + 1) * rows, :] = q_ref[:, head * HD : (head + 1) * HD]
        key = buf[0, 0, :, g * HD : (g + 1) * HD]
        value = buf[0, 0, :, (KVH + g) * HD : (KVH + g + 1) * HD]
        s = lax.dot_general(q_s[g], key, (((1,), (1,)), ((), ())), preferred_element_type=jnp.float32)
        s = s + tri
        m = jnp.max(s, axis=1, keepdims=True)
        p = jnp.exp2((s - m) * scale)
        top[g] = jnp.broadcast_to(m, (GROUP * rows, HD))
        total = jnp.sum(p, axis=1, keepdims=True)
        lane = lax.broadcasted_iota(jnp.int32, (GROUP * rows, HD), 1)
        tot[g] = jnp.where(lane == 0, total, 0.0)
        acc[g] = jnp.dot(p.astype(jnp.bfloat16), value, preferred_element_type=jnp.float32)

    keys = TILE * rows

    def attend(side, tile):
        at = pl.ds(tile * TILE, TILE)
        bias = bias_ref[side * steps + tile]
        for g in range(KVH):
            key = buf[side, at, :, g * HD : (g + 1) * HD].reshape(keys, HD)
            value = buf[side, at, :, (KVH + g) * HD : (KVH + g + 1) * HD].reshape(keys, HD)
            s = lax.dot_general(
                q_s[g], key, (((1,), (1,)), ((), ())), preferred_element_type=jnp.float32
            )
            s = s + bias
            m_old = top[g]
            m = jnp.maximum(m_old, jnp.max(s, axis=1, keepdims=True))
            factor = jnp.exp2((m_old - m) * scale)
            m_wide = jnp.concatenate([m] * (keys // HD), axis=1)
            p = jnp.exp2((s - m_wide) * scale)
            part = p[:, :HD]
            for b in range(1, keys // HD):
                part = part + p[:, b * HD : (b + 1) * HD]
            top[g] = m
            tot[g] = tot[g] * factor + part
            acc[g] = acc[g] * factor + jnp.dot(
                p.astype(jnp.bfloat16), value, preferred_element_type=jnp.float32
            )

    def step(j, carry):
        for flow in (0, 1):
            for jj in range(steps):

                @pl.when((core == flow) & (j == jj))
                def _():
                    for dst, count, todo, sem in flows[flow][2][jj]:
                        pltpu.make_async_remote_copy(
                            src_ref=buf.at[0, pl.ds(dst, count)],
                            dst_ref=buf.at[0, pl.ds(dst, count)],
                            send_sem=send_sem.at[0],
                            recv_sem=recv_sem.at[sem],
                            device_id=partner,
                            device_id_type=MESH,
                        ).wait_recv()
                        for send in todo:
                            ring_copy(flow, send).start()

        pair_copy(j).start()
        attend(0, j)

        @pl.when(j > 0)
        def _():
            pair_copy(j - 1).wait_recv()
            attend(1, j - 1)

        return carry

    lax.fori_loop(0, steps, step, 0)
    pair_copy(steps - 1).wait_recv()
    attend(1, steps - 1)

    chips = n_x * n_z
    pltpu.make_async_remote_copy(
        src_ref=buf.at[0, pl.ds(0, chips - 1)],
        dst_ref=buf.at[0, pl.ds(0, chips - 1)],
        send_sem=send_sem.at[0],
        recv_sem=recv_sem.at[0],
        device_id=partner,
        device_id_type=MESH,
    ).wait_send()
    pltpu.make_async_remote_copy(
        src_ref=buf.at[0, pl.ds(0, chips)],
        dst_ref=buf.at[1, pl.ds(0, chips)],
        send_sem=pair_send.at[0],
        recv_sem=recv_sem.at[0],
        device_id=partner,
        device_id_type=MESH,
    ).wait_send()

    me = (x * n_z + z) * 2 + core
    position = span_ref[me] * rows + lax.broadcasted_iota(jnp.int32, (rows, HD), 0)
    live = position < limit_ref[0]
    for g in range(KVH):
        for h in range(GROUP):
            head = g * GROUP + h
            at = slice(h * rows, (h + 1) * rows)
            total = jnp.sum(tot[g, at, :], axis=1, keepdims=True)
            result = jnp.where(live, acc[g, at, :] / total, 0.0)
            out_ref[:, head * HD : (head + 1) * HD] = result.astype(jnp.bfloat16)


def prompt_attention(prompt_query, prompt_key, prompt_value, prompt_length, span_order):
    rows = prompt_query.shape[0]
    n_x, n_z = lax.axis_size("seq_0"), lax.axis_size("seq_1")
    x, z, core = lax.axis_index("seq_0"), lax.axis_index("seq_1"), lax.axis_index("head")
    flow_a = build_flow(n_x, n_z)
    flow_b = build_flow(n_z, n_x)
    flows = (flow_a, flow_b)
    steps = len(flow_a[2])
    off = np.array(
        [[[a, b] for a, b in flow_a[0]], [[b, a] for a, b in flow_b[0]]], np.int32
    )
    order = jnp.where(core == 0, off, off[::-1])
    which = jnp.stack([core, 1 - core]).astype(jnp.int32)
    at_x = (order[..., 0] + x + n_x) % n_x
    at_z = (order[..., 1] + z + n_z) % n_z
    index = ((at_x * n_z + at_z) * 2 + which[:, None]).reshape(-1)
    me = (x * n_z + z) * 2 + core
    numbers = jnp.arange(span_order.shape[0], dtype=jnp.int32)
    picked = jnp.sum(jnp.where(index[:, None] == numbers[None, :], span_order[None, :], 0), axis=1)
    own = jnp.sum(jnp.where(me == numbers, span_order, 0))
    bias = jnp.where(picked < own, 0.0, NEG).astype(jnp.float32)
    bias = jnp.broadcast_to(bias[:, None], (bias.shape[0], rows)).reshape(2 * steps, 1, TILE * rows)
    width = 2 * KVH * HD
    sems = max(flow_a[3], flow_b[3])
    return pl.pallas_call(
        lambda *refs: prompt_kernel(flows, (n_x, n_z), *refs),
        out_shape=jax.ShapeDtypeStruct(prompt_query.shape, jnp.bfloat16),
        in_specs=[
            pl.BlockSpec(memory_space=pltpu.SMEM),
            pl.BlockSpec(memory_space=pltpu.SMEM),
            pl.BlockSpec(memory_space=pltpu.VMEM),
            pl.BlockSpec(memory_space=pltpu.VMEM),
            pl.BlockSpec(memory_space=pl.ANY),
            pl.BlockSpec(memory_space=pl.ANY),
        ],
        out_specs=pl.BlockSpec(memory_space=pltpu.VMEM),
        scratch_shapes=[
            pltpu.VMEM((2, n_x * n_z, rows, width), jnp.bfloat16),
            pltpu.VMEM((KVH, GROUP * rows, HD), jnp.bfloat16),
            pltpu.VMEM((KVH, GROUP * rows, HD), jnp.float32),
            pltpu.VMEM((KVH, GROUP * rows, HD), jnp.float32),
            pltpu.VMEM((KVH, GROUP * rows, HD), jnp.float32),
            pltpu.SemaphoreType.DMA((2,)),
            pltpu.SemaphoreType.DMA((sems,)),
            pltpu.SemaphoreType.DMA((1,)),
            pltpu.SemaphoreType.DMA((steps,)),
            pltpu.SemaphoreType.DMA((1,)),
        ],
        compiler_params=pltpu.CompilerParams(
            collective_id=0, has_side_effects=True, vmem_limit_bytes=48 * 1024 * 1024
        ),
        name="prompt_attention",
    )(span_order, prompt_length, prompt_query, bias, prompt_key, prompt_value)


def gathered_once(array, axis):
    leaves = jax.tree.leaves(array)
    order = sorted(range(len(leaves)), key=lambda k: -leaves[k].size)
    width = (1, *leaves[order[0]].shape)[-1]
    lines = [
        jnp.pad(leaves[k].reshape(-1), (0, -leaves[k].size % width)).reshape(-1, width)
        for k in order
    ]
    both, at, found = (lax.all_gather(jnp.concatenate(lines), axis), 0, {})
    for k, line in zip(order, lines):
        piece = both[:, at : at + len(line)].reshape(len(both), -1)
        found[k] = piece[:, : leaves[k].size].reshape(-1, *leaves[k].shape)
        at += len(line)
    numbers = iter(range(len(leaves)))
    return jax.tree.map(lambda _: found[next(numbers)], array)


def combined_by_axis(array, axes, combine):
    for axis in axes:
        pieces = gathered_once(array, axis)
        array = jax.tree.map(lambda part: part[0], pieces)
        for k in range(1, lax.axis_size(axis)):
            array = combine(array, jax.tree.map(lambda part: part[k], pieces))
    return array


def combine_parts(left, right):
    left_max, left_total, left_weighted = left
    right_max, right_total, right_weighted = right
    joint = jnp.maximum(left_max, right_max)
    left_factor = jnp.exp(left_max - joint)
    right_factor = jnp.exp(right_max - joint)
    return (
        joint,
        left_total * left_factor + right_total * right_factor,
        left_weighted * left_factor[..., None] + right_weighted * right_factor[..., None],
    )


def per_device(
    prompt_query,
    prompt_key,
    prompt_value,
    prompt_length,
    span_order,
    new_query,
    new_key,
    new_value,
    cache_key,
    cache_value,
    cache_length,
):
    head_group = QH // KVH
    score_scale = 1.0 / math.sqrt(HD)
    prompt_attended = prompt_attention(
        prompt_query, prompt_key, prompt_value, prompt_length, span_order
    )
    sessions = new_query.shape[0]
    local_heads = cache_key.shape[1]
    local_ctx = cache_key.shape[2]
    dec_queries = new_query.reshape(sessions, local_heads, head_group, HD)
    cache_pos = lax.axis_index(SEQ) * local_ctx + jnp.arange(local_ctx, dtype=jnp.int32)
    valid = (cache_pos[None, :] < cache_length[:, None])[:, None, None, :]
    scores = (
        jnp.einsum("skgd,sktd->skgt", dec_queries, cache_key, preferred_element_type=jnp.float32)
        * score_scale
    )
    scores = jnp.where(valid, scores, -1e30)
    row_max = jnp.max(scores, axis=-1)
    weights = jnp.where(valid, jnp.exp(scores - row_max[..., None]), 0.0)
    row_total = jnp.sum(weights, axis=-1)
    weighted = jnp.einsum(
        "skgt,sktd->skgd",
        weights.astype(jnp.bfloat16),
        cache_value,
        preferred_element_type=jnp.float32,
    )
    row_max, row_total, weighted = combined_by_axis(
        (row_max, row_total, weighted), SEQ, combine_parts
    )
    own_score = (
        jnp.einsum(
            "skgd,skd->skg",
            dec_queries,
            new_key.reshape(sessions, local_heads, HD),
            preferred_element_type=jnp.float32,
        )
        * score_scale
    )
    final_max = jnp.maximum(row_max, own_score)
    old_factor = jnp.exp(row_max - final_max)
    own_weight = jnp.exp(own_score - final_max)
    row_total = row_total * old_factor + own_weight
    own_rounded = lax.optimization_barrier(own_weight.astype(jnp.bfloat16)).astype(jnp.float32)
    fresh_value = new_value.reshape(sessions, local_heads, 1, HD).astype(jnp.float32)
    weighted = weighted * old_factor[..., None] + own_rounded[..., None] * fresh_value
    decode_attended = (weighted / row_total[..., None]).reshape(sessions, -1).astype(jnp.bfloat16)
    return (prompt_attended, decode_attended)


def solution(mesh):
    finer = Mesh(
        mesh.devices.reshape(mesh.shape["rep"], 8, 16, mesh.shape["head"]),
        ("rep", "seq_0", "seq_1", "head"),
    )
    placed = (
        P(REP_SEQ_HEAD, None),
        P(REP_SEQ_HEAD, None),
        P(REP_SEQ_HEAD, None),
        P("rep"),
        P("rep"),
        P("rep", "head"),
        P("rep", "head"),
        P("rep", "head"),
        P("rep", "head", SEQ, None),
        P("rep", "head", SEQ, None),
        P("rep"),
    )
    return jax.shard_map(
        per_device,
        mesh=finer,
        in_specs=placed,
        out_specs=(P(REP_SEQ_HEAD, None), P("rep", "head")),
        check_vma=False,
    )
```

time: 463 us -> 192 us (0.41)
  local copies, waits for them, and re-layouts: 106 us -> 14.9 us
  waiting for transfers between devices: 87.8 us -> 0 us
  Pallas kernels: 0 us -> 78.4 us
  other arithmetic: 76.8 us -> 6.73 us
  loops' own time: 41.9 us -> 0 us
  matrix products: 41.2 us -> 0.89 us
  between operations: 15.1 us -> 1.62 us
    all_gather x1 -> x0, waiting for transfers between devices: 87.8 us -> none  [side_by_side(): lax.all_gather(both, axis, axis=dim, tiled=True)]
    pallas_call x0 -> x1, Pallas kernels: none -> 78.4 us  [prompt_attention(): pl.pallas_call(lambda *refs: prompt_kernel(flows, (n_x, n_z), *refs), out...]
    dynamic_slice x64 -> x0, local copies, waits for them, and re-layouts: 61.8 us -> none  [the longest x32 43 us: advance(): lax.dynamic_slice_in_dim(values_piece, first_row, block_rows, 0)]
    another operation x33 -> x0, loops' own time: 41.9 us -> none  [the longest x1 40.1 us: attend_rows(): lax.scan(advance, running, jnp.arange(key_count // block_rows, dtype=jnp....]
    dot_general x64 -> x0, matrix products: 39.1 us -> none  [the longest x32 23.8 us: compute(): jnp.einsum('kgrn,nkd->kgrd', weights.astype(jnp.bfloat16), value_block, p...]
    reduce_sum x65 -> x2, other arithmetic: 27.3 us -> 0.81 us  [the longest x1 0.63 us: prompt_attention(): own = jnp.sum(jnp.where(me == numbers, span_order, 0))]
    while x3 -> x0, local copies, waits for them, and re-layouts: 23.9 us -> none  [attend_rows(): lax.scan(advance, running, jnp.arange(key_count // block_rows, dtype=jnp....]
    and x32 -> x0, other arithmetic: 23.2 us -> none  [advance(): (key_pos[None, :] <= query_pos[:, None]) & (key_pos[None, :] < length_limit)]
  transfers between devices with their start and end apart: 1 -> 0, of which waited for: 1 -> 0; matrix products, arithmetic and copies ran while one was open for 3% -> 0% of each run, Pallas kernels for 0% -> 0%
where the time goes in v1:
time: 192 us; the launch traced here: 191 us
  blocking collectives  89 us (46%)
  Pallas kernels  78.4 us (41%)
  local copies, waits for them, and re-layouts  14.9 us (8%)
  other arithmetic  6.73 us (4%)
    all_gather x2, blocking collectives, gathered_once(): both, at, found = (lax.all_gather(jnp.concatenate(lines), axis), 0, {})  89 us
    pallas_call x1, Pallas kernels, prompt_attention(): pl.pallas_call(lambda *refs: prompt_kernel(flows, (n_x, n_z), *refs), out...  78.4 us
    squeeze x45, local copies, waits for them, and re-layouts, combined_by_axis(): array = combine(array, jax.tree.map(lambda part: part[k], pieces))  8.41 us

profile of v1, /device:TPU:65, one launch (start us, length us, event | category | flops | bytes accessed | tf_op | source)
XLA Modules:
  0.0 191.5 jit_solution(8434731161106876627)
XLA Ops:
  0.7 0.9 broadcast_compare_fusion
  1.5 0.8 reshape.2590
  2.4 0.5 fusion.95
  2.8 0.2 fusion.4
  3.2 0.3 fusion.1
  3.6 21.5 %all-gather.2 = f32[8,114,128]{2,1,0:T(8,128)S(1)} all-gather(f32[1,114,128]{2,1,0:T(8,128)S(1)} %maximum_bitcast_fusion), channel_id=2, replica_groups=mesh['rep'=2,'seq_0'=8,'seq_1'=16,'head'=2] {'seq_0'}, dimensions={0}, use_global_device_ids=true | all-gather | bytes 525312 | tf_op jit(solution)/shard_map/all_gather | solution.py:356
  25.2 0.3 fusion.27
  25.5 67.4 %all-gather.3 = f32[16,114,128]{2,1,0:T(8,128)S(1)} all-gather(f32[1,114,128]{2,1,0:T(8,128)S(1)} %maximum_bitcast_fusion.1), channel_id=3, replica_groups=mesh['rep'=2,'seq_0'=8,'seq_1'=16,'head'=2] {'seq_1'}, dimensions={0}, use_global_device_ids=true | all-gather | bytes 992256 | tf_op jit(solution)/shard_map/all_gather | solution.py:356
  93.1 0.6 squeeze.257
  93.8 0.6 squeeze.259
  94.4 0.6 squeeze.261
  95.0 0.6 squeeze.263
  95.7 0.6 squeeze.265
  96.3 0.6 squeeze.267
  96.9 0.6 squeeze.269
  97.5 0.6 squeeze.271
  98.2 0.6 squeeze.273
  100.3 0.6 copy-done.9
  100.9 0.1 fusion.49
  102.6 0.1 multiply_add_fusion
  105.3 0.1 copy.21
  105.5 0.7 copy.22
  106.2 0.8 broadcast_multiply_fusion
  107.0 2.1 %fusion.10 = bf16[16,896]{1,0:T(8,128)(2,1)} fusion(f32[2,8,7,128]{3,2,1,0:T(8,128)S(1)} %bitcast.461, f32[2,8,7,128]{3,2,1,0:T(8,128)S(1)} %bitcast.456, f32[2,8,7,128]{3,2,1,0:T(8,128)S(1)} %bitcast.460, f32[16,896]{1,0:T(8,128)} %squeeze.273, f32[2,8,7,128]{3,2,1,0:T(8,128)S(1)} %bitcast.459, f32[2,8,7,128]{3,2,1,0:T(8,128)S(1)} %bitcast.458, ...), kind=kLoop, calls=%fused_computation.16 | loop fusion | flops 702464 | bytes 2838528 | tf_op jit(solution)/shard_map/convert_element_type | solution.py:444
  109.1 0.7 broadcast_select_fusion
  109.9 0.2 select_reduce_fusion
  110.1 0.6 fusion.53
  110.8 0.6 compare_select_fusion.4
  111.5 0.1 broadcast_in_dim.48
  111.6 0.1 broadcast_in_dim.49.refs_3_
  112.4 78.4 %prompt_attention.1 = bf16[64,1792]{1,0:T(8,128)(2,1)S(1)} custom-call(s32[256]{0:T(256)S(1)} %copy-done.4, s32[1]{0:T(128)S(6)} %copy.94.refs_1_, bf16[64,1792]{1,0:T(8,128)(2,1)S(1)} %copy-done.1, f32[32,1,512]{2,1,0:T(1,128)S(1)} %broadcast_in_dim.49.refs_3_, bf16[64,256]{1,0:T(8,128)(2,1)S(1)} %copy-done.2, bf16[64,256]{1,0:T(8,128)(2,1)S(1)} %copy-done.3), custom_call_target="tpu_custom_call" | custom-call | tf_op jit(solution)/shard_map/prompt_attention/pallas_call | solution.py:317
  190.8 0.7 copy.95
  (112 shorter events, 6.4 us)
Async XLA Ops:
  0.6 1.7 copy-start
  0.6 2.6 %copy-start.5 = (bf16[16,1,256,128]{3,2,1,0:T(8,128)(2,1)S(1)}, bf16[16,1,256,128]{3,2,1,0:T(8,128)(2,1)}, u32[]{:S(2)}) copy-start(bf16[16,1,256,128]{3,2,1,0:T(8,128)(2,1)} %param.22) | copy-start | bytes 3145732
  100.2 0.7 copy-start.9
  105.5 0.7 copy-start.7
  106.2 0.8 copy-start.6
  107.0 2.2 %copy-start.8 = (s32[2,128,2]{1,0,2:T(2,128)S(1)}, s32[2,128,2]{1,0,2:T(2,128)}, u32[]{:S(2)}) copy-start(s32[2,128,2]{1,0,2:T(2,128)} %constant.64.clone) | copy-start | bytes 6148
  107.0 2.9 %copy-start.4 = (s32[256]{0:T(256)S(1)}, s32[256]{0:T(256)}, u32[]{:S(2)}) copy-start(s32[256]{0:T(256)} %refs_0_.1) | copy-start | bytes 3076
  109.1 3.3 %copy-start.1 = (bf16[64,1792]{1,0:T(8,128)(2,1)S(1)}, bf16[64,1792]{1,0:T(8,128)(2,1)}, u32[]{:S(2)}) copy-start(bf16[64,1792]{1,0:T(8,128)(2,1)} %refs_2_.1) | copy-start | bytes 688132
  111.6 0.8 copy-start.2
  111.6 0.8 copy-start.3

commit v2 on v1

--- a/solution.py
+++ b/solution.py
@@ -1,3 +1,4 @@
+import functools
 import heapq
 import math
 
@@ -106,7 +107,7 @@
     return offsets, resolve(first), steps, len(events)
 
 
-def prompt_kernel(
+def attention_kernel(
     flows,
     sizes,
     span_ref,
@@ -115,17 +116,39 @@
     bias_ref,
     k_ref,
     v_ref,
+    len_ref,
+    nq_ref,
+    nk_ref,
+    nv_ref,
+    ck_ref,
+    cv_ref,
     out_ref,
+    dec_ref,
     buf,
     q_s,
     acc,
     top,
     tot,
+    ck,
+    cv,
+    q_dec,
+    p_dec,
+    stat,
+    part,
+    got1,
+    mine1,
+    got2,
+    mine2,
+    got3,
+    last,
+    got4,
     local_sem,
     recv_sem,
     send_sem,
     pair_recv,
     pair_send,
+    dec_recv,
+    dec_send,
 ):
     n_x, n_z = sizes
     rows = q_ref.shape[0]
@@ -143,6 +166,10 @@
     in_v = pltpu.make_async_copy(v_ref, buf.at[0, 0, :, KVH * HD :], local_sem.at[1])
     in_k.start()
     in_v.start()
+    in_ck = pltpu.make_async_copy(ck_ref.at[:, 0], ck, local_sem.at[2])
+    in_cv = pltpu.make_async_copy(cv_ref.at[:, 0], cv, local_sem.at[3])
+    in_ck.start()
+    in_cv.start()
     barrier = pltpu.get_barrier_semaphore()
     for dim in (0, 1):
         for way in (1, -1):
@@ -228,24 +255,194 @@
                 p.astype(jnp.bfloat16), value, preferred_element_type=jnp.float32
             )
 
+    sessions, ctx = ck_ref.shape[0], ck_ref.shape[2]
+    tall = sessions * 8
+    share = sessions // n_x
+    quad = math.isqrt(n_z)
+    first_chip = (x == 0) & (z == 0)
+    at_row = lax.broadcasted_iota(jnp.int32, (sessions, 8, HD), 1)
+    at_lane = lax.broadcasted_iota(jnp.int32, (sessions, 8, HD), 2)
+
+    def spread(h):
+        r = lax.broadcasted_iota(jnp.int32, (tall, sessions), 0)
+        c = lax.broadcasted_iota(jnp.int32, (tall, sessions), 1)
+        return jnp.where(r == c * 8 + h, 1.0, 0.0).astype(jnp.bfloat16)
+
+    def pack(m, l, o):
+        n = o.shape[0]
+        row_n, lane_n = at_row[:n], at_lane[:n]
+        line = jnp.where(lane_n == row_n, m, 0.0) + jnp.where(lane_n == row_n + 8, l, 0.0)
+        line = jnp.sum(line, axis=1, keepdims=True)
+        return jnp.where(row_n == 7, line, o)
+
+    def combine(tiles):
+        n = tiles[0].shape[0]
+        row_n, lane_n = at_row[:n], at_lane[:n]
+        tops, totals = [], []
+        for t in tiles:
+            line = jnp.broadcast_to(t[:, 7:8, :], t.shape)
+            tops.append(jnp.sum(jnp.where(lane_n == row_n, line, 0.0), axis=2, keepdims=True))
+            totals.append(jnp.sum(jnp.where(lane_n == row_n + 8, line, 0.0), axis=2, keepdims=True))
+        m = functools.reduce(jnp.maximum, tops)
+        l, o = 0.0, 0.0
+        for t, t_top, t_total in zip(tiles, tops, totals):
+            f = jnp.exp2((t_top - m) * scale)
+            l = l + t_total * f
+            o = o + t * f
+        return m, l, o
+
+    def decode_scores():
+        q_all = 0.0
+        for h in range(GROUP):
+            q_all = q_all + jnp.dot(
+                spread(h), nq_ref[:, h * HD : (h + 1) * HD], preferred_element_type=jnp.float32
+            )
+        q_dec[...] = q_all.reshape(sessions, 8, HD)
+        in_ck.wait()
+        begin = (x * n_z + z) * ctx
+        spot = lax.broadcasted_iota(jnp.int32, (8, ctx), 1) + begin
+        scores, valid, own = [], [], []
+        for s_id in range(sessions):
+            q_one = q_dec[s_id]
+            scores.append(
+                lax.dot_general(
+                    q_one.astype(jnp.bfloat16),
+                    ck[s_id],
+                    (((1,), (1,)), ((), ())),
+                    preferred_element_type=jnp.float32,
+                )
+            )
+            valid.append(jnp.where(spot < len_ref[s_id], 0.0, NEG))
+            own.append(q_one * nk_ref[s_id : s_id + 1, :].astype(jnp.float32))
+        bar = jnp.concatenate(valid, axis=0)
+        s = jnp.concatenate(scores, axis=0) + bar
+        own = jnp.sum(jnp.concatenate(own, axis=0), axis=1, keepdims=True)
+        own = jnp.where(first_chip, own, NEG)
+        m = jnp.maximum(jnp.max(s, axis=1, keepdims=True), own)
+        p = jnp.where(bar < 0.0, 0.0, jnp.exp2((s - m) * scale))
+        p_own = jnp.where(first_chip, jnp.exp2((own - m) * scale), 0.0)
+        total = jnp.sum(p, axis=1, keepdims=True) + p_own
+        p_dec[...] = p.reshape(sessions, 8, ctx)
+        stat[0] = jnp.broadcast_to(m, (tall, HD))
+        stat[1] = jnp.broadcast_to(total, (tall, HD))
+        stat[2] = jnp.broadcast_to(p_own, (tall, HD))
+
+    def decode_values():
+        in_cv.wait()
+        outs = []
+        for s_id in range(sessions):
+            o = jnp.dot(
+                p_dec[s_id].astype(jnp.bfloat16), cv[s_id], preferred_element_type=jnp.float32
+            )
+            extra = stat[2, s_id * 8 : (s_id + 1) * 8, :].astype(jnp.bfloat16).astype(jnp.float32)
+            outs.append(o + extra * nv_ref[s_id : s_id + 1, :].astype(jnp.float32))
+        o = jnp.concatenate(outs, axis=0).reshape(sessions, 8, HD)
+        m = stat[0].reshape(sessions, 8, HD)
+        total = stat[1].reshape(sessions, 8, HD)
+        part[...] = pack(m, total, o).reshape(part.shape)
+
+    def exchange(number, src, dst, sem, to):
+        return pltpu.make_async_remote_copy(
+            src_ref=src,
+            dst_ref=dst,
+            send_sem=dec_send.at[number],
+            recv_sem=dec_recv.at[sem],
+            device_id=to,
+            device_id_type=MESH,
+        )
+
+    base2, base3, base4 = n_x, n_x + quad, n_x + 2 * quad
+
+    def round1(d):
+        to = lax.rem(x + d, n_x)
+        return exchange(0, part.at[to], got1.at[d - 1], d, {"seq_0": to})
+
+    def round2(d):
+        to = (z // quad) * quad + lax.rem(lax.rem(z, quad) + d, quad)
+        return exchange(1, mine1, got2.at[d - 1], base2 + d, {"seq_1": to})
+
+    def round3(d):
+        to = lax.rem(z + d * quad, n_z)
+        return exchange(2, mine2, got3.at[d - 1], base3 + d, {"seq_1": to})
+
+    def round4(d):
+        to = lax.rem(x + d, n_x)
+        return exchange(3, last, got4.at[d - 1], base4 + d, {"seq_0": to})
+
+    def decode_round(j):
+        @pl.when(j == 3)
+        def _():
+            for d in range(1, n_x):
+                round1(d).start()
+
+        @pl.when(j == 5)
+        def _():
+            for d in range(1, n_x):
+                round1(d).wait_recv()
+            mine1[...] = pack(*combine([part[x]] + [got1[d - 1] for d in range(1, n_x)]))
+
+        @pl.when(j == 6)
+        def _():
+            for d in range(1, quad):
+                round2(d).start()
+
+        @pl.when(j == 8)
+        def _():
+            for d in range(1, quad):
+                round2(d).wait_recv()
+            mine2[...] = pack(*combine([mine1[...]] + [got2[d - 1] for d in range(1, quad)]))
+
+        @pl.when(j == 10)
+        def _():
+            for d in range(1, quad):
+                round3(d).start()
+
+        @pl.when(j == 13)
+        def _():
+            for d in range(1, quad):
+                round3(d).wait_recv()
+            _, l, o = combine([mine2[...]] + [got3[d - 1] for d in range(1, quad)])
+            last[...] = jnp.where(at_row[:share] == 7, 0.0, o / l)
+
+        @pl.when(j == 14)
+        def _():
+            for d in range(1, n_x):
+                round4(d).start()
+
+    def receive(flow, arrivals):
+        for dst, count, todo, sem in arrivals:
+            pltpu.make_async_remote_copy(
+                src_ref=buf.at[0, pl.ds(dst, count)],
+                dst_ref=buf.at[0, pl.ds(dst, count)],
+                send_sem=send_sem.at[0],
+                recv_sem=recv_sem.at[sem],
+                device_id=partner,
+                device_id_type=MESH,
+            ).wait_recv()
+            for send in todo:
+                ring_copy(flow, send).start()
+
     def step(j, carry):
+        @pl.when(j == 0)
+        def _():
+            for lo, hi, work in ((0, 2, decode_scores), (2, 4, decode_values), (4, None, None)):
+                for flow in (0, 1):
+
+                    @pl.when(core == flow)
+                    def _():
+                        receive(flow, flows[flow][2][0][lo:hi])
+
+                if work is not None:
+                    work()
+
         for flow in (0, 1):
-            for jj in range(steps):
+            for jj in range(1, steps):
 
                 @pl.when((core == flow) & (j == jj))
                 def _():
-                    for dst, count, todo, sem in flows[flow][2][jj]:
-                        pltpu.make_async_remote_copy(
-                            src_ref=buf.at[0, pl.ds(dst, count)],
-                            dst_ref=buf.at[0, pl.ds(dst, count)],
-                            send_sem=send_sem.at[0],
-                            recv_sem=recv_sem.at[sem],
-                            device_id=partner,
-                            device_id_type=MESH,
-                        ).wait_recv()
-                        for send in todo:
-                            ring_copy(flow, send).start()
-
+                    receive(flow, flows[flow][2][jj])
+
+        decode_round(j)
         pair_copy(j).start()
         attend(0, j)
 
@@ -260,6 +457,26 @@
     pair_copy(steps - 1).wait_recv()
     attend(1, steps - 1)
 
+    for d in range(1, n_x):
+        round4(d).wait_recv()
+    got4[n_x - 1] = last[...]
+    final = got4[...].reshape(tall, HD).astype(jnp.bfloat16)
+    for h in range(GROUP):
+        r = lax.broadcasted_iota(jnp.int32, (sessions, tall), 0)
+        c = lax.broadcasted_iota(jnp.int32, (sessions, tall), 1)
+        owner = lax.rem(x - 1 - c // (8 * share) + 2 * n_x, n_x)
+        pick = (owner == r // share) & (lax.rem(c // 8, share) == lax.rem(r, share))
+        pick = jnp.where(pick & (lax.rem(c, 8) == h), 1.0, 0.0).astype(jnp.bfloat16)
+        row = jnp.dot(pick, final, preferred_element_type=jnp.float32)
+        dec_ref[:, h * HD : (h + 1) * HD] = row.astype(jnp.bfloat16)
+
+    def drain(number, ref):
+        exchange(number, ref, ref, 0, partner).wait_send()
+
+    drain(0, got1)
+    drain(1, got2)
+    drain(2, got3)
+    drain(3, got4.at[pl.ds(0, n_x - 1)])
     chips = n_x * n_z
     pltpu.make_async_remote_copy(
         src_ref=buf.at[0, pl.ds(0, chips - 1)],
@@ -290,7 +507,19 @@
             out_ref[:, head * HD : (head + 1) * HD] = result.astype(jnp.bfloat16)
 
 
-def prompt_attention(prompt_query, prompt_key, prompt_value, prompt_length, span_order):
+def per_device(
+    prompt_query,
+    prompt_key,
+    prompt_value,
+    prompt_length,
+    span_order,
+    new_query,
+    new_key,
+    new_value,
+    cache_key,
+    cache_value,
+    cache_length,
+):
     rows = prompt_query.shape[0]
     n_x, n_z = lax.axis_size("seq_0"), lax.axis_size("seq_1")
     x, z, core = lax.axis_index("seq_0"), lax.axis_index("seq_1"), lax.axis_index("head")
@@ -314,9 +543,14 @@
     bias = jnp.broadcast_to(bias[:, None], (bias.shape[0], rows)).reshape(2 * steps, 1, TILE * rows)
     width = 2 * KVH * HD
     sems = max(flow_a[3], flow_b[3])
+    sessions, ctx = cache_key.shape[0], cache_key.shape[2]
+    share, quad = sessions // n_x, math.isqrt(n_z)
     return pl.pallas_call(
-        lambda *refs: prompt_kernel(flows, (n_x, n_z), *refs),
-        out_shape=jax.ShapeDtypeStruct(prompt_query.shape, jnp.bfloat16),
+        lambda *refs: attention_kernel(flows, (n_x, n_z), *refs),
+        out_shape=(
+            jax.ShapeDtypeStruct(prompt_query.shape, jnp.bfloat16),
+            jax.ShapeDtypeStruct(new_query.shape, jnp.bfloat16),
+        ),
         in_specs=[
             pl.BlockSpec(memory_space=pltpu.SMEM),
             pl.BlockSpec(memory_space=pltpu.SMEM),
@@ -324,125 +558,62 @@
             pl.BlockSpec(memory_space=pltpu.VMEM),
             pl.BlockSpec(memory_space=pl.ANY),
             pl.BlockSpec(memory_space=pl.ANY),
+            pl.BlockSpec(memory_space=pltpu.SMEM),
+            pl.BlockSpec(memory_space=pltpu.VMEM),
+            pl.BlockSpec(memory_space=pltpu.VMEM),
+            pl.BlockSpec(memory_space=pltpu.VMEM),
+            pl.BlockSpec(memory_space=pl.ANY),
+            pl.BlockSpec(memory_space=pl.ANY),
         ],
-        out_specs=pl.BlockSpec(memory_space=pltpu.VMEM),
+        out_specs=(
+            pl.BlockSpec(memory_space=pltpu.VMEM),
+            pl.BlockSpec(memory_space=pltpu.VMEM),
+        ),
         scratch_shapes=[
             pltpu.VMEM((2, n_x * n_z, rows, width), jnp.bfloat16),
             pltpu.VMEM((KVH, GROUP * rows, HD), jnp.bfloat16),
             pltpu.VMEM((KVH, GROUP * rows, HD), jnp.float32),
             pltpu.VMEM((KVH, GROUP * rows, HD), jnp.float32),
             pltpu.VMEM((KVH, GROUP * rows, HD), jnp.float32),
-            pltpu.SemaphoreType.DMA((2,)),
+            pltpu.VMEM((sessions, ctx, HD), jnp.bfloat16),
+            pltpu.VMEM((sessions, ctx, HD), jnp.bfloat16),
+            pltpu.VMEM((sessions, 8, HD), jnp.float32),
+            pltpu.VMEM((sessions, 8, ctx), jnp.float32),
+            pltpu.VMEM((3, sessions * 8, HD), jnp.float32),
+            pltpu.VMEM((n_x, share, 8, HD), jnp.float32),
+            pltpu.VMEM((n_x - 1, share, 8, HD), jnp.float32),
+            pltpu.VMEM((share, 8, HD), jnp.float32),
+            pltpu.VMEM((quad - 1, share, 8, HD), jnp.float32),
+            pltpu.VMEM((share, 8, HD), jnp.float32),
+            pltpu.VMEM((quad - 1, share, 8, HD), jnp.float32),
+            pltpu.VMEM((share, 8, HD), jnp.float32),
+            pltpu.VMEM((n_x, share, 8, HD), jnp.float32),
+            pltpu.SemaphoreType.DMA((4,)),
             pltpu.SemaphoreType.DMA((sems,)),
             pltpu.SemaphoreType.DMA((1,)),
             pltpu.SemaphoreType.DMA((steps,)),
             pltpu.SemaphoreType.DMA((1,)),
+            pltpu.SemaphoreType.DMA((2 * n_x + 2 * quad,)),
+            pltpu.SemaphoreType.DMA((4,)),
         ],
         compiler_params=pltpu.CompilerParams(
             collective_id=0, has_side_effects=True, vmem_limit_bytes=48 * 1024 * 1024
         ),
-        name="prompt_attention",
-    )(span_order, prompt_length, prompt_query, bias, prompt_key, prompt_value)
-
-
-def gathered_once(array, axis):
-    leaves = jax.tree.leaves(array)
-    order = sorted(range(len(leaves)), key=lambda k: -leaves[k].size)
-    width = (1, *leaves[order[0]].shape)[-1]
-    lines = [
-        jnp.pad(leaves[k].reshape(-1), (0, -leaves[k].size % width)).reshape(-1, width)
-        for k in order
-    ]
-    both, at, found = (lax.all_gather(jnp.concatenate(lines), axis), 0, {})
-    for k, line in zip(order, lines):
-        piece = both[:, at : at + len(line)].reshape(len(both), -1)
-        found[k] = piece[:, : leaves[k].size].reshape(-1, *leaves[k].shape)
-        at += len(line)
-    numbers = iter(range(len(leaves)))
-    return jax.tree.map(lambda _: found[next(numbers)], array)
-
-
-def combined_by_axis(array, axes, combine):
-    for axis in axes:
-        pieces = gathered_once(array, axis)
-        array = jax.tree.map(lambda part: part[0], pieces)
-        for k in range(1, lax.axis_size(axis)):
-            array = combine(array, jax.tree.map(lambda part: part[k], pieces))
-    return array
-
-
-def combine_parts(left, right):
-    left_max, left_total, left_weighted = left
-    right_max, right_total, right_weighted = right
-    joint = jnp.maximum(left_max, right_max)
-    left_factor = jnp.exp(left_max - joint)
-    right_factor = jnp.exp(right_max - joint)
-    return (
-        joint,
-        left_total * left_factor + right_total * right_factor,
-        left_weighted * left_factor[..., None] + right_weighted * right_factor[..., None],
+        name="prefill_decode_attention",
+    )(
+        span_order,
+        prompt_length,
+        prompt_query,
+        bias,
+        prompt_key,
+        prompt_value,
+        cache_length,
+        new_query,
+        new_key,
+        new_value,
+        cache_key,
+        cache_value,
     )
-
-
-def per_device(
-    prompt_query,
-    prompt_key,
-    prompt_value,
-    prompt_length,
-    span_order,
-    new_query,
-    new_key,
-    new_value,
-    cache_key,
-    cache_value,
-    cache_length,
-):
-    head_group = QH // KVH
-    score_scale = 1.0 / math.sqrt(HD)
-    prompt_attended = prompt_attention(
-        prompt_query, prompt_key, prompt_value, prompt_length, span_order
-    )
-    sessions = new_query.shape[0]
-    local_heads = cache_key.shape[1]
-    local_ctx = cache_key.shape[2]
-    dec_queries = new_query.reshape(sessions, local_heads, head_group, HD)
-    cache_pos = lax.axis_index(SEQ) * local_ctx + jnp.arange(local_ctx, dtype=jnp.int32)
-    valid = (cache_pos[None, :] < cache_length[:, None])[:, None, None, :]
-    scores = (
-        jnp.einsum("skgd,sktd->skgt", dec_queries, cache_key, preferred_element_type=jnp.float32)
-        * score_scale
-    )
-    scores = jnp.where(valid, scores, -1e30)
-    row_max = jnp.max(scores, axis=-1)
-    weights = jnp.where(valid, jnp.exp(scores - row_max[..., None]), 0.0)
-    row_total = jnp.sum(weights, axis=-1)
-    weighted = jnp.einsum(
-        "skgt,sktd->skgd",
-        weights.astype(jnp.bfloat16),
-        cache_value,
-        preferred_element_type=jnp.float32,
-    )
-    row_max, row_total, weighted = combined_by_axis(
-        (row_max, row_total, weighted), SEQ, combine_parts
-    )
-    own_score = (
-        jnp.einsum(
-            "skgd,skd->skg",
-            dec_queries,
-            new_key.reshape(sessions, local_heads, HD),
-            preferred_element_type=jnp.float32,
-        )
-        * score_scale
-    )
-    final_max = jnp.maximum(row_max, own_score)
-    old_factor = jnp.exp(row_max - final_max)
-    own_weight = jnp.exp(own_score - final_max)
-    row_total = row_total * old_factor + own_weight
-    own_rounded = lax.optimization_barrier(own_weight.astype(jnp.bfloat16)).astype(jnp.float32)
-    fresh_value = new_value.reshape(sessions, local_heads, 1, HD).astype(jnp.float32)
-    weighted = weighted * old_factor[..., None] + own_rounded[..., None] * fresh_value
-    decode_attended = (weighted / row_total[..., None]).reshape(sessions, -1).astype(jnp.bfloat16)
-    return (prompt_attended, decode_attended)
 
 
 def solution(mesh):

time: 192 us -> 122 us (0.64)
  blocking collectives: 89 us -> 0 us
  Pallas kernels: 78.4 us -> 113 us
  local copies, waits for them, and re-layouts: 14.9 us -> 4.66 us
  other arithmetic: 6.73 us -> 3.11 us
    all_gather x2 -> x0, blocking collectives: 89 us -> none  [gathered_once(): both, at, found = (lax.all_gather(jnp.concatenate(lines), axis), 0, {})]
    pallas_call x1, Pallas kernels: 78.4 us -> 113 us  [per_device(): pl.pallas_call(lambda *refs: attention_kernel(flows, (n_x, n_z), *refs),...]
    squeeze x48 -> x0, local copies, waits for them, and re-layouts: 8.59 us -> none  [the longest x45 8.41 us: combined_by_axis(): array = combine(array, jax.tree.map(lambda part: part[k], pieces))]
    mul x32 -> x0, local copies, waits for them, and re-layouts: 3.27 us -> none  [the longest x15 1.25 us: combine_parts(): left_weighted * left_factor[..., None]]
    unnamed x21 -> x24, local copies, waits for them, and re-layouts: 1.39 us -> 4.35 us
    convert_element_type x3 -> x0, other arithmetic: 2.11 us -> none  [the longest x1 2.07 us: per_device(): (weighted / row_total[..., None]).reshape(sessions, -1).astype(jnp.bfloat16)]
where the time goes in v2:
time: 122 us
  Pallas kernels  113 us (93%)
  local copies, waits for them, and re-layouts  4.66 us (4%)
  other arithmetic  3.11 us (3%)
  between operations  1.47 us (1%)
    pallas_call x1, Pallas kernels, per_device(): pl.pallas_call(lambda *refs: attention_kernel(flows, (n_x, n_z), *refs),...  113 us
    unnamed x24, local copies, waits for them, and re-layouts  4.35 us

profile of v2, /device:TPU:65, one launch (start us, length us, event | category | flops | bytes accessed | tf_op | source)
XLA Modules:
  0.0 121.9 jit_solution(13368004474551581279)
XLA Ops:
  0.6 0.0 copy-start.10
  0.6 0.0 copy-start.2
  1.4 1.4 %fusion.2 = s32[]{:T(128)} fusion(s32[256]{0:T(256)} %refs_0_.1, s32[]{:T(128)S(6)} %add.109), kind=kLoop, calls=%fused_computation.13 | loop fusion | flops 767 | bytes 1032 | tf_op jit(solution)/shard_map/reduce_sum | solution.py:541
  2.8 0.1 pad_add_fusion
  2.8 0.0 copy-done.10
  2.8 0.1 bitcast_add_fusion
  2.9 0.9 select_reduce_fusion
  3.8 0.7 compare_select_fusion.4
  4.5 0.1 select_n.53
  4.6 0.1 broadcast_in_dim.37
  4.7 0.0 copy-start.3
  4.7 0.0 copy-start.4
  4.7 0.0 copy-start.5
  4.7 0.0 copy-start.6
  4.7 0.0 copy-start.7
  4.7 0.0 copy-start.8
  4.7 0.0 copy-start.9
  4.7 0.1 broadcast_in_dim.38.refs_3_
  4.9 0.0 copy-done.2
  4.9 0.5 copy-done.3
  5.4 0.0 copy-done.4
  5.4 0.0 copy-done.5
  5.5 0.0 copy-done.6
  5.5 0.0 copy-done.7
  5.5 0.0 copy-done.8
  5.5 0.0 copy-done.9
  5.5 0.0 copy-start
  5.5 1.2 copy-done
  6.7 1.2 %copy-done.1 = bf16[16,1,256,128]{3,2,1,0:T(8,128)(2,1)S(1)} copy-done((bf16[16,1,256,128]{3,2,1,0:T(8,128)(2,1)S(1)}, bf16[16,1,256,128]{3,2,1,0:T(8,128)(2,1)}, u32[]{:S(2)}) %copy-start.1) | copy-done | bytes 1048600
  7.9 112.7 %prefill_decode_attention.1 = (bf16[64,1792]{1,0:T(8,128)(2,1)S(1)}, bf16[16,896]{1,0:T(8,128)(2,1)S(1)}) custom-call(s32[256]{0:T(256)S(1)} %copy-done.6, s32[1]{0:T(128)S(6)} %copy.17.refs_1_, bf16[64,1792]{1,0:T(8,128)(2,1)S(1)} %copy-done.2, f32[32,1,512]{2,1,0:T(1,128)S(1)} %broadcast_in_dim.38.refs_3_, bf16[64,256]{1,0:T(8,128)(2,1)S(1)} %copy-done.3, ...), custom_call_target="tpu_custom_call" | custom-call | tf_op jit(solution)/shard_map/prefill_decode_attention/pallas_call | solution.py:548
  120.6 0.7 copy.18
  121.3 0.6 copy.19
  (2 shorter events, 0.0 us)
Async XLA Ops:
  0.6 2.2 %copy-start.10 = (s32[2,128,2]{1,0,2:T(2,128)S(1)}, s32[2,128,2]{1,0,2:T(2,128)}, u32[]{:S(2)}) copy-start(s32[2,128,2]{1,0,2:T(2,128)} %constant.57.clone) | copy-start | bytes 6148
  0.6 4.2 %copy-start.2 = (bf16[64,1792]{1,0:T(8,128)(2,1)S(1)}, bf16[64,1792]{1,0:T(8,128)(2,1)}, u32[]{:S(2)}) copy-start(bf16[64,1792]{1,0:T(8,128)(2,1)} %refs_2_.1) | copy-start | bytes 688132
  4.7 0.8 copy-start.3
  4.7 0.8 copy-start.4
  4.7 0.8 copy-start.5
  4.7 0.8 copy-start.6
  4.7 0.7 copy-start.7
  4.7 0.7 copy-start.8
  4.7 0.7 copy-start.9
  5.5 1.2 %copy-start = (bf16[16,1,256,128]{3,2,1,0:T(8,128)(2,1)S(1)}, bf16[16,1,256,128]{3,2,1,0:T(8,128)(2,1)}, u32[]{:S(2)}) copy-start(bf16[16,1,256,128]{3,2,1,0:T(8,128)(2,1)} %refs_10_.1) | copy-start | bytes 3145732
  6.7 1.2 %copy-start.1 = (bf16[16,1,256,128]{3,2,1,0:T(8,128)(2,1)S(1)}, bf16[16,1,256,128]{3,2,1,0:T(8,128)(2,1)}, u32[]{:S(2)}) copy-start(bf16[16,1,256,128]{3,2,1,0:T(8,128)(2,1)} %refs_11_.1) | copy-start | bytes 3145732

commit v3 on v2

--- a/solution.py
+++ b/solution.py
@@ -112,19 +112,23 @@
     sizes,
     span_ref,
     limit_ref,
-    q_ref,
-    bias_ref,
+    place_ref,
+    q_hbm,
     k_ref,
     v_ref,
     len_ref,
-    nq_ref,
-    nk_ref,
-    nv_ref,
+    nq_hbm,
+    nk_hbm,
+    nv_hbm,
     ck_ref,
     cv_ref,
     out_ref,
     dec_ref,
     buf,
+    q_ref,
+    nq_ref,
+    nk_ref,
+    nv_ref,
     q_s,
     acc,
     top,
@@ -168,8 +172,16 @@
     in_v.start()
     in_ck = pltpu.make_async_copy(ck_ref.at[:, 0], ck, local_sem.at[2])
     in_cv = pltpu.make_async_copy(cv_ref.at[:, 0], cv, local_sem.at[3])
+    in_q = pltpu.make_async_copy(q_hbm, q_ref, local_sem.at[4])
+    in_new = [
+        pltpu.make_async_copy(src, dst, local_sem.at[5 + i])
+        for i, (src, dst) in enumerate(((nq_hbm, nq_ref), (nk_hbm, nk_ref), (nv_hbm, nv_ref)))
+    ]
+    in_q.start()
     in_ck.start()
     in_cv.start()
+    for copy in in_new:
+        copy.start()
     barrier = pltpu.get_barrier_semaphore()
     for dim in (0, 1):
         for way in (1, -1):
@@ -210,6 +222,7 @@
 
     scale = math.log2(math.e) / math.sqrt(HD)
 
+    in_q.wait()
     row = lax.broadcasted_iota(jnp.int32, (rows, rows), 0)
     col = lax.broadcasted_iota(jnp.int32, (rows, rows), 1)
     tri = jnp.concatenate([jnp.where(col <= row, 0.0, NEG).astype(jnp.float32)] * GROUP, axis=0)
@@ -230,10 +243,23 @@
         acc[g] = jnp.dot(p.astype(jnp.bfloat16), value, preferred_element_type=jnp.float32)
 
     keys = TILE * rows
+    own_span = span_ref[(x * n_z + z) * 2 + core]
 
     def attend(side, tile):
         at = pl.ds(tile * TILE, TILE)
-        bias = bias_ref[side * steps + tile]
+        flow = core if side == 0 else 1 - core
+        marks = []
+        for b in range(TILE):
+            slot = flow * n_x * n_z + tile * TILE + b
+            at_x = lax.rem(x + place_ref[slot], n_x)
+            at_z = lax.rem(z + place_ref[2 * n_x * n_z + slot], n_z)
+            span = span_ref[(at_x * n_z + at_z) * 2 + flow]
+            marks.append(jnp.where(span < own_span, 0.0, NEG).astype(jnp.float32))
+        lane = lax.broadcasted_iota(jnp.int32, (1, HD), 1)
+        bias = []
+        for b in range(0, TILE, 2):
+            bias.append(jnp.where(lane < rows, marks[b], marks[b + 1]))
+        bias = jnp.concatenate(bias, axis=1)
         for g in range(KVH):
             key = buf[side, at, :, g * HD : (g + 1) * HD].reshape(keys, HD)
             value = buf[side, at, :, (KVH + g) * HD : (KVH + g + 1) * HD].reshape(keys, HD)
@@ -292,6 +318,8 @@
         return m, l, o
 
     def decode_scores():
+        for copy in in_new:
+            copy.wait()
         q_all = 0.0
         for h in range(GROUP):
             q_all = q_all + jnp.dot(
@@ -370,32 +398,25 @@
         return exchange(3, last, got4.at[d - 1], base4 + d, {"seq_0": to})
 
     def decode_round(j):
-        @pl.when(j == 3)
+        @pl.when(j == 5)
         def _():
-            for d in range(1, n_x):
-                round1(d).start()
-
-        @pl.when(j == 5)
+            decode_scores()
+
+        @pl.when(j == 6)
+        def _():
+            decode_values()
+
+        @pl.when(j == 8)
         def _():
             for d in range(1, n_x):
                 round1(d).wait_recv()
             mine1[...] = pack(*combine([part[x]] + [got1[d - 1] for d in range(1, n_x)]))
 
-        @pl.when(j == 6)
-        def _():
-            for d in range(1, quad):
-                round2(d).start()
-
-        @pl.when(j == 8)
+        @pl.when(j == 10)
         def _():
             for d in range(1, quad):
                 round2(d).wait_recv()
             mine2[...] = pack(*combine([mine1[...]] + [got2[d - 1] for d in range(1, quad)]))
-
-        @pl.when(j == 10)
-        def _():
-            for d in range(1, quad):
-                round3(d).start()
 
         @pl.when(j == 13)
         def _():
@@ -404,10 +425,13 @@
             _, l, o = combine([mine2[...]] + [got3[d - 1] for d in range(1, quad)])
             last[...] = jnp.where(at_row[:share] == 7, 0.0, o / l)
 
-        @pl.when(j == 14)
-        def _():
-            for d in range(1, n_x):
-                round4(d).start()
+    def decode_send(j):
+        for at, one_round, count in ((6, round1, n_x), (8, round2, quad), (10, round3, quad), (13, round4, n_x)):
+
+            @pl.when(j == at)
+            def _():
+                for d in range(1, count):
+                    one_round(d).start()
 
     def receive(flow, arrivals):
         for dst, count, todo, sem in arrivals:
@@ -423,20 +447,8 @@
                 ring_copy(flow, send).start()
 
     def step(j, carry):
-        @pl.when(j == 0)
-        def _():
-            for lo, hi, work in ((0, 2, decode_scores), (2, 4, decode_values), (4, None, None)):
-                for flow in (0, 1):
-
-                    @pl.when(core == flow)
-                    def _():
-                        receive(flow, flows[flow][2][0][lo:hi])
-
-                if work is not None:
-                    work()
-
         for flow in (0, 1):
-            for jj in range(1, steps):
+            for jj in range(steps):
 
                 @pl.when((core == flow) & (j == jj))
                 def _():
@@ -451,6 +463,7 @@
             pair_copy(j - 1).wait_recv()
             attend(1, j - 1)
 
+        decode_send(j)
         return carry
 
     lax.fori_loop(0, steps, step, 0)
@@ -522,25 +535,13 @@
 ):
     rows = prompt_query.shape[0]
     n_x, n_z = lax.axis_size("seq_0"), lax.axis_size("seq_1")
-    x, z, core = lax.axis_index("seq_0"), lax.axis_index("seq_1"), lax.axis_index("head")
     flow_a = build_flow(n_x, n_z)
     flow_b = build_flow(n_z, n_x)
     flows = (flow_a, flow_b)
     steps = len(flow_a[2])
-    off = np.array(
-        [[[a, b] for a, b in flow_a[0]], [[b, a] for a, b in flow_b[0]]], np.int32
-    )
-    order = jnp.where(core == 0, off, off[::-1])
-    which = jnp.stack([core, 1 - core]).astype(jnp.int32)
-    at_x = (order[..., 0] + x + n_x) % n_x
-    at_z = (order[..., 1] + z + n_z) % n_z
-    index = ((at_x * n_z + at_z) * 2 + which[:, None]).reshape(-1)
-    me = (x * n_z + z) * 2 + core
-    numbers = jnp.arange(span_order.shape[0], dtype=jnp.int32)
-    picked = jnp.sum(jnp.where(index[:, None] == numbers[None, :], span_order[None, :], 0), axis=1)
-    own = jnp.sum(jnp.where(me == numbers, span_order, 0))
-    bias = jnp.where(picked < own, 0.0, NEG).astype(jnp.float32)
-    bias = jnp.broadcast_to(bias[:, None], (bias.shape[0], rows)).reshape(2 * steps, 1, TILE * rows)
+    place_x = [a % n_x for a, _ in flow_a[0]] + [b % n_x for _, b in flow_b[0]]
+    place_z = [b % n_z for _, b in flow_a[0]] + [a % n_z for a, _ in flow_b[0]]
+    places = jnp.asarray(np.array(place_x + place_z, np.int32))
     width = 2 * KVH * HD
     sems = max(flow_a[3], flow_b[3])
     sessions, ctx = cache_key.shape[0], cache_key.shape[2]
@@ -551,26 +552,20 @@
             jax.ShapeDtypeStruct(prompt_query.shape, jnp.bfloat16),
             jax.ShapeDtypeStruct(new_query.shape, jnp.bfloat16),
         ),
-        in_specs=[
-            pl.BlockSpec(memory_space=pltpu.SMEM),
-            pl.BlockSpec(memory_space=pltpu.SMEM),
-            pl.BlockSpec(memory_space=pltpu.VMEM),
-            pl.BlockSpec(memory_space=pltpu.VMEM),
-            pl.BlockSpec(memory_space=pl.ANY),
-            pl.BlockSpec(memory_space=pl.ANY),
-            pl.BlockSpec(memory_space=pltpu.SMEM),
-            pl.BlockSpec(memory_space=pltpu.VMEM),
-            pl.BlockSpec(memory_space=pltpu.VMEM),
-            pl.BlockSpec(memory_space=pltpu.VMEM),
-            pl.BlockSpec(memory_space=pl.ANY),
-            pl.BlockSpec(memory_space=pl.ANY),
-        ],
+        in_specs=[pl.BlockSpec(memory_space=pltpu.SMEM)] * 3
+        + [pl.BlockSpec(memory_space=pltpu.HBM)] * 3
+        + [pl.BlockSpec(memory_space=pltpu.SMEM)]
+        + [pl.BlockSpec(memory_space=pltpu.HBM)] * 5,
         out_specs=(
             pl.BlockSpec(memory_space=pltpu.VMEM),
             pl.BlockSpec(memory_space=pltpu.VMEM),
         ),
         scratch_shapes=[
             pltpu.VMEM((2, n_x * n_z, rows, width), jnp.bfloat16),
+            pltpu.VMEM(prompt_query.shape, jnp.bfloat16),
+            pltpu.VMEM(new_query.shape, jnp.bfloat16),
+            pltpu.VMEM(new_key.shape, jnp.bfloat16),
+            pltpu.VMEM(new_value.shape, jnp.bfloat16),
             pltpu.VMEM((KVH, GROUP * rows, HD), jnp.bfloat16),
             pltpu.VMEM((KVH, GROUP * rows, HD), jnp.float32),
             pltpu.VMEM((KVH, GROUP * rows, HD), jnp.float32),
@@ -588,7 +583,7 @@
             pltpu.VMEM((quad - 1, share, 8, HD), jnp.float32),
             pltpu.VMEM((share, 8, HD), jnp.float32),
             pltpu.VMEM((n_x, share, 8, HD), jnp.float32),
-            pltpu.SemaphoreType.DMA((4,)),
+            pltpu.SemaphoreType.DMA((8,)),
             pltpu.SemaphoreType.DMA((sems,)),
             pltpu.SemaphoreType.DMA((1,)),
             pltpu.SemaphoreType.DMA((steps,)),
@@ -597,14 +592,14 @@
             pltpu.SemaphoreType.DMA((4,)),
         ],
         compiler_params=pltpu.CompilerParams(
-            collective_id=0, has_side_effects=True, vmem_limit_bytes=48 * 1024 * 1024
+            collective_id=0, has_side_effects=True, vmem_limit_bytes=67_000_000
         ),
         name="prefill_decode_attention",
     )(
         span_order,
         prompt_length,
+        places,
         prompt_query,
-        bias,
         prompt_key,
         prompt_value,
         cache_length,

time: 122 us -> 118 us (0.967)
  other arithmetic: 3.11 us -> 0 us
  local copies, waits for them, and re-layouts: 4.66 us -> 2.26 us
    reduce_sum x2 -> x0, other arithmetic: 2.25 us -> none  [the longest x1 1.4 us: per_device(): own = jnp.sum(jnp.where(me == numbers, span_order, 0))]
    unnamed x24 -> x4, local copies, waits for them, and re-layouts: 4.35 us -> 2.26 us
    pallas_call x1, Pallas kernels: 113 us -> 114 us  [per_device(): pl.pallas_call(lambda *refs: attention_kernel(flows, (n_x, n_z), *refs),...]
where the time goes in v3:
time: 118 us
  Pallas kernels  114 us (97%)
  local copies, waits for them, and re-layouts  2.26 us (2%)
  between operations  1.3 us (1%)
    pallas_call x1, Pallas kernels, per_device(): pl.pallas_call(lambda *refs: attention_kernel(flows, (n_x, n_z), *refs),...  114 us

profile of v3, /device:TPU:65, one launch (start us, length us, event | category | flops | bytes accessed | tf_op | source)
XLA Modules:
  0.0 117.8 jit_solution(17723041084116271203)
XLA Ops:
  1.3 114.3 %prefill_decode_attention.1 = (bf16[64,1792]{1,0:T(8,128)(2,1)}, bf16[16,896]{1,0:T(8,128)(2,1)}) custom-call(s32[256]{0:T(256)} %refs_0_.1, s32[1]{0:T(128)S(6)} %copy.16.refs_1_, s32[512]{0:T(512)} %constant.2.clone.refs_2_, bf16[64,1792]{1,0:T(8,128)(2,1)} %refs_3_.1, bf16[64,256]{1,0:T(8,128)(2,1)} %refs_4_.1, bf16[64,256]{1,0:T(8,128)(2,1)} %refs_5_.1, ...), custom_call_target="tpu_custom_call" | custom-call | tf_op jit(solution)/shard_map/prefill_decode_attention/pallas_call | solution.py:549
  115.6 0.0 copy-start
  115.6 1.6 %copy.17 = bf16[64,1792]{1,0:T(8,128)(2,1)} copy(bf16[64,1792]{1,0:T(8,128)(2,1)} %get-tuple-element.4) | data formatting | bytes 458752
  117.2 0.0 copy-done
  117.2 0.6 copy.18
Async XLA Ops:
  115.6 1.7 %copy-start = (bf16[16,896]{1,0:T(8,128)(2,1)S(1)}, bf16[16,896]{1,0:T(8,128)(2,1)}, u32[]{:S(2)}) copy-start(bf16[16,896]{1,0:T(8,128)(2,1)} %get-tuple-element.5) | copy-start | bytes 86020

commit v4 on v3

--- a/solution.py
+++ b/solution.py
@@ -35,7 +35,7 @@
         begin = max(now, free.get(link, 0.0))
         free[link] = begin + units * (0.75 if link[0] == 2 else 1.4)
         seq[0] += 1
-        heapq.heappush(heap, (free[link] + 2.5, seq[0], item))
+        heapq.heappush(heap, (free[link] + 4.0, seq[0], item))
         into.append(item)
 
     def phase2(now, k, into):
@@ -91,11 +91,11 @@
             out.append((ring, way, src, dst, count, number[item]))
         return out
 
-    steps, total = [], len(offsets) // TILE
+    steps, total = [], 2 * len(offsets) // TILE
     events = [(place(item), resolve(sends[item]), number[item]) for item in order]
     at, filled = 0, {0}
-    for tile in range(total):
-        need = set(range(tile * TILE, (tile + 1) * TILE))
+    for half in range(total):
+        need = set(range(half * TILE // 2, (half + 1) * TILE // 2))
         mine = []
         while not need <= filled:
             (dst, count), todo, sem = events[at]
@@ -110,13 +110,13 @@
 def attention_kernel(
     flows,
     sizes,
-    span_ref,
+    span_hbm,
     limit_ref,
-    place_ref,
+    place_hbm,
     q_hbm,
     k_ref,
     v_ref,
-    len_ref,
+    len_hbm,
     nq_hbm,
     nk_hbm,
     nv_hbm,
@@ -125,6 +125,9 @@
     out_ref,
     dec_ref,
     buf,
+    span_ref,
+    place_ref,
+    len_ref,
     q_ref,
     nq_ref,
     nk_ref,
@@ -157,7 +160,7 @@
     n_x, n_z = sizes
     rows = q_ref.shape[0]
     x, z, core = lax.axis_index("seq_0"), lax.axis_index("seq_1"), lax.axis_index("head")
-    steps = len(flows[0][2])
+    steps = len(flows[0][2]) // 2
     names = ("seq_0", "seq_1")
     here = (x, z)
     extent = (n_x, n_z)
@@ -166,6 +169,11 @@
         return {names[dim]: lax.rem(here[dim] + way + extent[dim], extent[dim])}
 
     partner = {"head": 1 - core}
+    barrier = pltpu.get_barrier_semaphore()
+    for dim in (0, 1):
+        for way in (1, -1):
+            pl.semaphore_signal(barrier, inc=1, device_id=target(dim, way), device_id_type=MESH)
+    pl.semaphore_signal(barrier, inc=1, device_id=partner, device_id_type=MESH)
     in_k = pltpu.make_async_copy(k_ref, buf.at[0, 0, :, : KVH * HD], local_sem.at[0])
     in_v = pltpu.make_async_copy(v_ref, buf.at[0, 0, :, KVH * HD :], local_sem.at[1])
     in_k.start()
@@ -177,16 +185,19 @@
         pltpu.make_async_copy(src, dst, local_sem.at[5 + i])
         for i, (src, dst) in enumerate(((nq_hbm, nq_ref), (nk_hbm, nk_ref), (nv_hbm, nv_ref)))
     ]
+    in_scalars = [
+        pltpu.make_async_copy(src, dst, local_sem.at[8 + i])
+        for i, (src, dst) in enumerate(
+            ((span_hbm, span_ref), (place_hbm, place_ref), (len_hbm, len_ref))
+        )
+    ]
     in_q.start()
+    for copy in in_scalars:
+        copy.start()
     in_ck.start()
     in_cv.start()
     for copy in in_new:
         copy.start()
-    barrier = pltpu.get_barrier_semaphore()
-    for dim in (0, 1):
-        for way in (1, -1):
-            pl.semaphore_signal(barrier, inc=1, device_id=target(dim, way), device_id_type=MESH)
-    pl.semaphore_signal(barrier, inc=1, device_id=partner, device_id_type=MESH)
     in_k.wait()
     in_v.wait()
     pl.semaphore_wait(barrier, 5)
@@ -203,12 +214,13 @@
             device_id_type=MESH,
         )
 
-    def pair_copy(tile):
+    def pair_copy(half):
+        at = pl.ds(half * (TILE // 2), TILE // 2)
         return pltpu.make_async_remote_copy(
-            src_ref=buf.at[0, pl.ds(tile * TILE, TILE)],
-            dst_ref=buf.at[1, pl.ds(tile * TILE, TILE)],
+            src_ref=buf.at[0, at],
+            dst_ref=buf.at[1, at],
             send_sem=pair_send.at[0],
-            recv_sem=pair_recv.at[tile],
+            recv_sem=pair_recv.at[half],
             device_id=partner,
             device_id_type=MESH,
         )
@@ -243,6 +255,8 @@
         acc[g] = jnp.dot(p.astype(jnp.bfloat16), value, preferred_element_type=jnp.float32)
 
     keys = TILE * rows
+    for copy in in_scalars:
+        copy.wait()
     own_span = span_ref[(x * n_z + z) * 2 + core]
 
     def attend(side, tile):
@@ -398,25 +412,40 @@
         return exchange(3, last, got4.at[d - 1], base4 + d, {"seq_0": to})
 
     def decode_round(j):
-        @pl.when(j == 5)
+        @pl.when(j == 1)
         def _():
             decode_scores()
 
+        @pl.when(j == 2)
+        def _():
+            decode_values()
+
+        @pl.when(j == 4)
+        def _():
+            for d in range(1, n_x):
+                round1(d).start()
+
         @pl.when(j == 6)
-        def _():
-            decode_values()
-
-        @pl.when(j == 8)
         def _():
             for d in range(1, n_x):
                 round1(d).wait_recv()
             mine1[...] = pack(*combine([part[x]] + [got1[d - 1] for d in range(1, n_x)]))
 
-        @pl.when(j == 10)
+        @pl.when(j == 7)
+        def _():
+            for d in range(1, quad):
+                round2(d).start()
+
+        @pl.when(j == 9)
         def _():
             for d in range(1, quad):
                 round2(d).wait_recv()
             mine2[...] = pack(*combine([mine1[...]] + [got2[d - 1] for d in range(1, quad)]))
+
+        @pl.when(j == 10)
+        def _():
+            for d in range(1, quad):
+                round3(d).start()
 
         @pl.when(j == 13)
         def _():
@@ -425,13 +454,10 @@
             _, l, o = combine([mine2[...]] + [got3[d - 1] for d in range(1, quad)])
             last[...] = jnp.where(at_row[:share] == 7, 0.0, o / l)
 
-    def decode_send(j):
-        for at, one_round, count in ((6, round1, n_x), (8, round2, quad), (10, round3, quad), (13, round4, n_x)):
-
-            @pl.when(j == at)
-            def _():
-                for d in range(1, count):
-                    one_round(d).start()
+        @pl.when(j == 14)
+        def _():
+            for d in range(1, n_x):
+                round4(d).start()
 
     def receive(flow, arrivals):
         for dst, count, todo, sem in arrivals:
@@ -446,28 +472,43 @@
             for send in todo:
                 ring_copy(flow, send).start()
 
+    def receive_block(flow, j, lo, hi):
+        if hi - lo == 1:
+            for half in (2 * lo, 2 * lo + 1):
+                receive(flow, flows[flow][2][half])
+                pair_copy(half).start()
+            return
+        mid = (lo + hi) // 2
+
+        @pl.when(j < mid)
+        def _():
+            receive_block(flow, j, lo, mid)
+
+        @pl.when(j >= mid)
+        def _():
+            receive_block(flow, j, mid, hi)
+
     def step(j, carry):
         for flow in (0, 1):
-            for jj in range(steps):
-
-                @pl.when((core == flow) & (j == jj))
-                def _():
-                    receive(flow, flows[flow][2][jj])
+
+            @pl.when(core == flow)
+            def _():
+                receive_block(flow, j, 0, steps)
 
         decode_round(j)
-        pair_copy(j).start()
         attend(0, j)
 
         @pl.when(j > 0)
         def _():
-            pair_copy(j - 1).wait_recv()
+            pair_copy(2 * j - 2).wait_recv()
+            pair_copy(2 * j - 1).wait_recv()
             attend(1, j - 1)
 
-        decode_send(j)
         return carry
 
     lax.fori_loop(0, steps, step, 0)
-    pair_copy(steps - 1).wait_recv()
+    pair_copy(2 * steps - 2).wait_recv()
+    pair_copy(2 * steps - 1).wait_recv()
     attend(1, steps - 1)
 
     for d in range(1, n_x):
@@ -538,7 +579,7 @@
     flow_a = build_flow(n_x, n_z)
     flow_b = build_flow(n_z, n_x)
     flows = (flow_a, flow_b)
-    steps = len(flow_a[2])
+    steps = len(flow_a[2]) // 2
     place_x = [a % n_x for a, _ in flow_a[0]] + [b % n_x for _, b in flow_b[0]]
     place_z = [b % n_z for _, b in flow_a[0]] + [a % n_z for a, _ in flow_b[0]]
     places = jnp.asarray(np.array(place_x + place_z, np.int32))
@@ -552,16 +593,18 @@
             jax.ShapeDtypeStruct(prompt_query.shape, jnp.bfloat16),
             jax.ShapeDtypeStruct(new_query.shape, jnp.bfloat16),
         ),
-        in_specs=[pl.BlockSpec(memory_space=pltpu.SMEM)] * 3
-        + [pl.BlockSpec(memory_space=pltpu.HBM)] * 3
-        + [pl.BlockSpec(memory_space=pltpu.SMEM)]
-        + [pl.BlockSpec(memory_space=pltpu.HBM)] * 5,
+        in_specs=[
+            pl.BlockSpec(memory_space=pltpu.SMEM if i == 1 else pltpu.HBM) for i in range(12)
+        ],
         out_specs=(
             pl.BlockSpec(memory_space=pltpu.VMEM),
             pl.BlockSpec(memory_space=pltpu.VMEM),
         ),
         scratch_shapes=[
             pltpu.VMEM((2, n_x * n_z, rows, width), jnp.bfloat16),
+            pltpu.SMEM(span_order.shape, jnp.int32),
+            pltpu.SMEM(places.shape, jnp.int32),
+            pltpu.SMEM(cache_length.shape, jnp.int32),
             pltpu.VMEM(prompt_query.shape, jnp.bfloat16),
             pltpu.VMEM(new_query.shape, jnp.bfloat16),
             pltpu.VMEM(new_key.shape, jnp.bfloat16),
@@ -583,31 +626,31 @@
             pltpu.VMEM((quad - 1, share, 8, HD), jnp.float32),
             pltpu.VMEM((share, 8, HD), jnp.float32),
             pltpu.VMEM((n_x, share, 8, HD), jnp.float32),
-            pltpu.SemaphoreType.DMA((8,)),
+            pltpu.SemaphoreType.DMA((11,)),
             pltpu.SemaphoreType.DMA((sems,)),
             pltpu.SemaphoreType.DMA((1,)),
-            pltpu.SemaphoreType.DMA((steps,)),
+            pltpu.SemaphoreType.DMA((2 * steps,)),
             pltpu.SemaphoreType.DMA((1,)),
             pltpu.SemaphoreType.DMA((2 * n_x + 2 * quad,)),
             pltpu.SemaphoreType.DMA((4,)),
         ],
         compiler_params=pltpu.CompilerParams(
-            collective_id=0, has_side_effects=True, vmem_limit_bytes=67_000_000
+            collective_id=0, has_side_effects=True, vmem_limit_bytes=55_000_000
         ),
         name="prefill_decode_attention",
     )(
-        span_order,
+        pltpu.with_memory_space_constraint(span_order, pltpu.HBM),
         prompt_length,
-        places,
-        prompt_query,
-        prompt_key,
-        prompt_value,
-        cache_length,
-        new_query,
-        new_key,
-        new_value,
-        cache_key,
-        cache_value,
+        pltpu.with_memory_space_constraint(places, pltpu.HBM),
+        pltpu.with_memory_space_constraint(prompt_query, pltpu.HBM),
+        pltpu.with_memory_space_constraint(prompt_key, pltpu.HBM),
+        pltpu.with_memory_space_constraint(prompt_value, pltpu.HBM),
+        pltpu.with_memory_space_constraint(cache_length, pltpu.HBM),
+        pltpu.with_memory_space_constraint(new_query, pltpu.HBM),
+        pltpu.with_memory_space_constraint(new_key, pltpu.HBM),
+        pltpu.with_memory_space_constraint(new_value, pltpu.HBM),
+        pltpu.with_memory_space_constraint(cache_key, pltpu.HBM),
+        pltpu.with_memory_space_constraint(cache_value, pltpu.HBM),
     )
 
 

time: 118 us -> 114 us (0.966)
  Pallas kernels: 114 us -> 111 us
    pallas_call x1, Pallas kernels: 114 us -> 111 us  [per_device(): pl.pallas_call(lambda *refs: attention_kernel(flows, (n_x, n_z), *refs),...]
where the time goes in v4:
time: 114 us
  Pallas kernels  111 us (97%)
  local copies, waits for them, and re-layouts  1.3 us (1%)
  between operations  1.29 us (1%)
    pallas_call x1, Pallas kernels, per_device(): pl.pallas_call(lambda *refs: attention_kernel(flows, (n_x, n_z), *refs),...  111 us

profile of v4, /device:TPU:65, one launch (start us, length us, event | category | flops | bytes accessed | tf_op | source)
XLA Modules:
  0.0 114.0 jit_solution(7908226223248537591)
XLA Ops:
  1.3 111.4 %prefill_decode_attention.1 = (bf16[64,1792]{1,0:T(8,128)(2,1)S(1)}, bf16[16,896]{1,0:T(8,128)(2,1)S(1)}) custom-call(s32[256]{0:T(256)} %refs_0_.1, s32[1]{0:T(128)S(6)} %copy.16.refs_1_, s32[512]{0:T(512)} %constant.2.clone.refs_2_, bf16[64,1792]{1,0:T(8,128)(2,1)} %refs_3_.1, bf16[64,256]{1,0:T(8,128)(2,1)} %refs_4_.1, bf16[64,256]{1,0:T(8,128)(2,1)} %refs_5_.1, ...), custom_call_target="tpu_custom_call" | custom-call | tf_op jit(solution)/shard_map/prefill_decode_attention/pallas_call | solution.py:590
  112.7 0.7 copy.17
  113.3 0.6 copy.18

commit v5 on v4

--- a/solution.py
+++ b/solution.py
@@ -204,7 +204,7 @@
 
     def ring_copy(flow, send):
         ring, way, src, dst, count, sem = send
-        dim = (ring - 1) if flow == 0 else (2 - ring)
+        dim = (2 - ring) if flow == 0 else (ring - 1)
         return pltpu.make_async_remote_copy(
             src_ref=buf.at[0, pl.ds(src, count)],
             dst_ref=buf.at[0, pl.ds(dst, count)],
@@ -331,33 +331,36 @@
             o = o + t * f
         return m, l, o
 
-    def decode_scores():
-        for copy in in_new:
-            copy.wait()
-        q_all = 0.0
-        for h in range(GROUP):
-            q_all = q_all + jnp.dot(
-                spread(h), nq_ref[:, h * HD : (h + 1) * HD], preferred_element_type=jnp.float32
+    halves = (range(sessions // 2), range(sessions // 2, sessions))
+
+    def decode_scores(part_of):
+        if part_of == 0:
+            for copy in in_new:
+                copy.wait()
+            q_all = 0.0
+            for h in range(GROUP):
+                q_all = q_all + jnp.dot(
+                    spread(h), nq_ref[:, h * HD : (h + 1) * HD], preferred_element_type=jnp.float32
+                )
+            q_dec[...] = q_all.reshape(sessions, 8, HD)
+            in_ck.wait()
+        for s_id in halves[part_of]:
+            p_dec[s_id] = lax.dot_general(
+                q_dec[s_id].astype(jnp.bfloat16),
+                ck[s_id],
+                (((1,), (1,)), ((), ())),
+                preferred_element_type=jnp.float32,
             )
-        q_dec[...] = q_all.reshape(sessions, 8, HD)
-        in_ck.wait()
+
+    def decode_softmax():
         begin = (x * n_z + z) * ctx
         spot = lax.broadcasted_iota(jnp.int32, (8, ctx), 1) + begin
-        scores, valid, own = [], [], []
+        valid, own = [], []
         for s_id in range(sessions):
-            q_one = q_dec[s_id]
-            scores.append(
-                lax.dot_general(
-                    q_one.astype(jnp.bfloat16),
-                    ck[s_id],
-                    (((1,), (1,)), ((), ())),
-                    preferred_element_type=jnp.float32,
-                )
-            )
             valid.append(jnp.where(spot < len_ref[s_id], 0.0, NEG))
-            own.append(q_one * nk_ref[s_id : s_id + 1, :].astype(jnp.float32))
+            own.append(q_dec[s_id] * nk_ref[s_id : s_id + 1, :].astype(jnp.float32))
         bar = jnp.concatenate(valid, axis=0)
-        s = jnp.concatenate(scores, axis=0) + bar
+        s = p_dec[...].reshape(tall, ctx) + bar
         own = jnp.sum(jnp.concatenate(own, axis=0), axis=1, keepdims=True)
         own = jnp.where(first_chip, own, NEG)
         m = jnp.maximum(jnp.max(s, axis=1, keepdims=True), own)
@@ -369,19 +372,23 @@
         stat[1] = jnp.broadcast_to(total, (tall, HD))
         stat[2] = jnp.broadcast_to(p_own, (tall, HD))
 
-    def decode_values():
-        in_cv.wait()
+    def decode_values(part_of):
+        if part_of == 0:
+            in_cv.wait()
         outs = []
-        for s_id in range(sessions):
+        for s_id in halves[part_of]:
             o = jnp.dot(
                 p_dec[s_id].astype(jnp.bfloat16), cv[s_id], preferred_element_type=jnp.float32
             )
             extra = stat[2, s_id * 8 : (s_id + 1) * 8, :].astype(jnp.bfloat16).astype(jnp.float32)
             outs.append(o + extra * nv_ref[s_id : s_id + 1, :].astype(jnp.float32))
-        o = jnp.concatenate(outs, axis=0).reshape(sessions, 8, HD)
-        m = stat[0].reshape(sessions, 8, HD)
-        total = stat[1].reshape(sessions, 8, HD)
-        part[...] = pack(m, total, o).reshape(part.shape)
+        n = sessions // 2
+        at = slice(part_of * n * 8, (part_of + 1) * n * 8)
+        o = jnp.concatenate(outs, axis=0).reshape(n, 8, HD)
+        m = stat[0, at, :].reshape(n, 8, HD)
+        total = stat[1, at, :].reshape(n, 8, HD)
+        to = slice(part_of * n_x // 2, (part_of + 1) * n_x // 2)
+        part[to] = pack(m, total, o).reshape(n_x // 2, share, 8, HD)
 
     def exchange(number, src, dst, sem, to):
         return pltpu.make_async_remote_copy(
@@ -411,53 +418,64 @@
         to = lax.rem(x + d, n_x)
         return exchange(3, last, got4.at[d - 1], base4 + d, {"seq_0": to})
 
+    def send_round(one_round, count):
+        for d in range(1, count):
+            one_round(d).start()
+
+    def wait_round(one_round, count):
+        for d in range(1, count):
+            one_round(d).wait_recv()
+
     def decode_round(j):
         @pl.when(j == 1)
         def _():
-            decode_scores()
+            decode_scores(0)
 
         @pl.when(j == 2)
         def _():
-            decode_values()
+            decode_scores(1)
+
+        @pl.when(j == 3)
+        def _():
+            decode_softmax()
+            decode_values(0)
 
         @pl.when(j == 4)
         def _():
-            for d in range(1, n_x):
-                round1(d).start()
-
-        @pl.when(j == 6)
-        def _():
-            for d in range(1, n_x):
-                round1(d).wait_recv()
+            decode_values(1)
+
+        @pl.when(j == 7)
+        def _():
+            wait_round(round1, n_x)
             mine1[...] = pack(*combine([part[x]] + [got1[d - 1] for d in range(1, n_x)]))
 
-        @pl.when(j == 7)
-        def _():
-            for d in range(1, quad):
-                round2(d).start()
-
         @pl.when(j == 9)
         def _():
-            for d in range(1, quad):
-                round2(d).wait_recv()
+            wait_round(round2, quad)
             mine2[...] = pack(*combine([mine1[...]] + [got2[d - 1] for d in range(1, quad)]))
 
         @pl.when(j == 10)
         def _():
-            for d in range(1, quad):
-                round3(d).start()
+            send_round(round3, quad)
 
         @pl.when(j == 13)
         def _():
-            for d in range(1, quad):
-                round3(d).wait_recv()
+            wait_round(round3, quad)
             _, l, o = combine([mine2[...]] + [got3[d - 1] for d in range(1, quad)])
             last[...] = jnp.where(at_row[:share] == 7, 0.0, o / l)
 
         @pl.when(j == 14)
         def _():
-            for d in range(1, n_x):
-                round4(d).start()
+            send_round(round4, n_x)
+
+    def decode_send(j):
+        @pl.when(j == 4)
+        def _():
+            send_round(round1, n_x)
+
+        @pl.when(j == 7)
+        def _():
+            send_round(round2, quad)
 
     def receive(flow, arrivals):
         for dst, count, todo, sem in arrivals:
@@ -504,13 +522,10 @@
             pair_copy(2 * j - 1).wait_recv()
             attend(1, j - 1)
 
+        decode_send(j)
         return carry
 
     lax.fori_loop(0, steps, step, 0)
-    pair_copy(2 * steps - 2).wait_recv()
-    pair_copy(2 * steps - 1).wait_recv()
-    attend(1, steps - 1)
-
     for d in range(1, n_x):
         round4(d).wait_recv()
     got4[n_x - 1] = last[...]
@@ -523,6 +538,10 @@
         pick = jnp.where(pick & (lax.rem(c, 8) == h), 1.0, 0.0).astype(jnp.bfloat16)
         row = jnp.dot(pick, final, preferred_element_type=jnp.float32)
         dec_ref[:, h * HD : (h + 1) * HD] = row.astype(jnp.bfloat16)
+
+    pair_copy(2 * steps - 2).wait_recv()
+    pair_copy(2 * steps - 1).wait_recv()
+    attend(1, steps - 1)
 
     def drain(number, ref):
         exchange(number, ref, ref, 0, partner).wait_send()
@@ -576,12 +595,12 @@
 ):
     rows = prompt_query.shape[0]
     n_x, n_z = lax.axis_size("seq_0"), lax.axis_size("seq_1")
-    flow_a = build_flow(n_x, n_z)
-    flow_b = build_flow(n_z, n_x)
+    flow_a = build_flow(n_z, n_x)
+    flow_b = build_flow(n_x, n_z)
     flows = (flow_a, flow_b)
     steps = len(flow_a[2]) // 2
-    place_x = [a % n_x for a, _ in flow_a[0]] + [b % n_x for _, b in flow_b[0]]
-    place_z = [b % n_z for _, b in flow_a[0]] + [a % n_z for a, _ in flow_b[0]]
+    place_x = [b % n_x for _, b in flow_a[0]] + [a % n_x for a, _ in flow_b[0]]
+    place_z = [a % n_z for a, _ in flow_a[0]] + [b % n_z for _, b in flow_b[0]]
     places = jnp.asarray(np.array(place_x + place_z, np.int32))
     width = 2 * KVH * HD
     sems = max(flow_a[3], flow_b[3])

time: 114 us -> 111 us (0.974)
  Pallas kernels: 111 us -> 108 us
    pallas_call x1, Pallas kernels: 111 us -> 108 us  [per_device(): pl.pallas_call(lambda *refs: attention_kernel(flows, (n_x, n_z), *refs),...]
where the time goes in v5:
time: 111 us; the launch traced here: 110 us
  Pallas kernels  108 us (97%)
  local copies, waits for them, and re-layouts  1.3 us (1%)
  between operations  1.29 us (1%)
    pallas_call x1, Pallas kernels, per_device(): pl.pallas_call(lambda *refs: attention_kernel(flows, (n_x, n_z), *refs),...  108 us

profile of v5, /device:TPU:65, one launch (start us, length us, event | category | flops | bytes accessed | tf_op | source)
XLA Modules:
  0.0 110.4 jit_solution(14488802739398653081)
XLA Ops:
  1.3 107.8 %prefill_decode_attention.1 = (bf16[64,1792]{1,0:T(8,128)(2,1)S(1)}, bf16[16,896]{1,0:T(8,128)(2,1)S(1)}) custom-call(s32[256]{0:T(256)} %refs_0_.1, s32[1]{0:T(128)S(6)} %copy.16.refs_1_, s32[512]{0:T(512)} %constant.2.clone.refs_2_, bf16[64,1792]{1,0:T(8,128)(2,1)} %refs_3_.1, bf16[64,256]{1,0:T(8,128)(2,1)} %refs_4_.1, bf16[64,256]{1,0:T(8,128)(2,1)} %refs_5_.1, ...), custom_call_target="tpu_custom_call" | custom-call | tf_op jit(solution)/shard_map/prefill_decode_attention/pallas_call | solution.py:609
  109.1 0.7 copy.17
  109.8 0.6 copy.18
